TPU v7x, 256 devices: a 8x8x2 block of a 8x8x16 slice. The times are simulated.
256 devices in a mesh: groups: 2 (over z), ep: 16 (over x, core), tp: 8 (over y).
Axes of the slice: x: 8, y: 8, z: 2, core: 2. Of those that a mesh axis runs over, the one named last changes fastest.
The devices are a block of a 8x8x16 slice.
Arguments:
- tokens: bfloat16 [1024, 7168], P(('groups', 'ep')), parts along dimension 0, may hold values from -6 to 6
- w_gate: bfloat16 [16, 7168, 2048], P('ep', None, 'tp'), may hold values from -0.0625 to 0.0625
- w_up: bfloat16 [16, 7168, 2048], P('ep', None, 'tp'), may hold values from -0.0625 to 0.0625
- w_down: bfloat16 [16, 2048, 7168], P('ep', 'tp'), may hold values from -0.1875 to 0.1875
- router_logits: float32 [1024, 8], P(('groups', 'ep')), parts along dimension 0, may hold values from -6 to 6
- expert_ids: int32 [1024, 8], P(('groups', 'ep')), parts along dimension 0, may hold values from 0 to 15, all different within a row; in each aligned block of 32 rows (0 to 31, 32 to 63, ...) at most 24 rows name the same one
- draft_lengths: int32 [128], P(('groups', 'ep')), parts along dimension 0, may hold values from 7 to 8
- accept_mask: int32 [128, 8], P(('groups', 'ep')), parts along dimension 0, may hold values 0 or 1
Outputs:
- mixed: bfloat16 [1024, 7168], P(('groups', 'ep'), 'tp'), parts along dimension 0
- accepted: int32 [2], P('groups'), parts along dimension 0
There are 2 independent parts, one for each index of `groups`. A program takes and returns all parts, laid end to end along the dimension named above; an argument that names none is the same for every part. Nothing has to cross between parts.
Inputs may be any that keep to these rules, and one draw needn't show every extreme that they name: `expert_ids`: each row names 8 different experts. Among the rows of one ep index (aligned blocks of 32 rows) no expert is named by more than 24 rows, and in every draw some expert is named by exactly 24 rows of some block.
All inputs are finite; a program needn't handle non-finite values. No bound on the sum of `accept_mask` on one device may be relied on, other than what follows from the above.
Results may differ from a plain program's by a relative error of at most 0.017.
Values may be sent and summed in bfloat16 or wider, within the bound.
No kernel may reach another device: no remote copies, remote signals or barrier semaphores. Data moves between devices by JAX's collectives and lax.ppermute only.
A program may use at most 128 MiB of HBM per device.

v0:
```python
import functools
import jax
import jax.numpy as jnp
from jax import lax
from jax.experimental import pallas as pl
from jax.experimental.pallas import tpu as pltpu
from jax.sharding import Mesh
from jax.sharding import PartitionSpec as P

DRAFT = 8
CORES = 2
EXTRA = 128
CHAINS = 2
F32 = jnp.float32
BF16 = jnp.bfloat16


VMEM = pl.BlockSpec(memory_space=pltpu.VMEM)
SMEM = pl.BlockSpec(memory_space=pltpu.SMEM)
HBM = pl.BlockSpec(memory_space=pltpu.HBM)


def payload_kernel(ep, lengths, mask, tokens, logits, ids, left):
    rows, half = tokens.shape
    top = ids.shape[1]
    left[:, :half] = tokens[...]
    row = lax.broadcasted_iota(jnp.int32, (rows, EXTRA), 0)
    lane = lax.broadcasted_iota(jnp.int32, (rows, EXTRA), 1)
    count = jnp.int32(0)
    live = jnp.zeros((rows, EXTRA), jnp.int32)
    for r in range(rows // DRAFT):
        prefix = jnp.int32(1)
        for j in range(DRAFT):
            prefix = prefix * mask[r, j] * (j < lengths[r]).astype(jnp.int32)
            count = count + prefix
        live = live + ((row >= r * DRAFT) & (row < r * DRAFT + lengths[r])).astype(jnp.int32)
    sig = 1.0 / (1.0 + jnp.exp(-logits[...]))
    gates = 2.827 * sig / jnp.sum(sig, axis=1, keepdims=True)
    dense = jnp.zeros((rows, EXTRA), F32)
    for k in range(top):
        dense = dense + jnp.where(ids[:, k:k + 1] == lax.rem(lane, ep), gates[:, k:k + 1], 0.0)
    dense = jnp.where(live > 0, dense, 0.0)
    high = dense.astype(BF16).astype(F32)
    extra = jnp.where(lane < ep, high, jnp.where(lane < 2 * ep, dense - high, 0.0))
    extra = jnp.where((lane == 2 * ep) & (row == 0), count.astype(F32), extra)
    left[:, half:] = extra.astype(BF16)


def payload(ep, tokens, logits, ids, lengths, mask):
    rows, half = tokens.shape
    return pl.pallas_call(
        functools.partial(payload_kernel, ep),
        in_specs=[SMEM, SMEM, VMEM, VMEM, VMEM],
        out_specs=VMEM,
        out_shape=jax.ShapeDtypeStruct((rows, half + EXTRA), BF16),
        compiler_params=pltpu.CompilerParams(vmem_limit_bytes=8 << 20),
    )(lengths, mask, tokens, logits, ids)


def gather_kernel(n, ep, order, place, *refs):
    lefts, rights = refs[:n], refs[n:2 * n]
    x, *gates, count = refs[2 * n:]
    rows = lefts[0].shape[0]
    half = rights[0].shape[1]
    lane = lax.broadcasted_iota(jnp.int32, (rows, EXTRA), 1)
    total = jnp.zeros((), F32)
    for i in range(n):
        at = pl.ds(pl.multiple_of(lax.rem(place[2] + order[i] % n, n) * rows, rows), rows)
        x[at, :half] = lefts[i][:, :half]
        x[at, half:] = rights[i][...]
        extra = lefts[i][:, half:].astype(F32)
        total = total + jnp.sum(jnp.where(lane == 2 * ep, extra, 0.0))
        for side in range(CORES):
            e = place[side]
            gate = jnp.sum(jnp.where((lane == e) | (lane == e + ep), extra, 0.0), axis=1, keepdims=True)
            gates[side][at, :] = jnp.broadcast_to(gate, (rows, gates[side].shape[1]))
    count[...] = jnp.full(count.shape, total, F32)


def gather(place, order, lefts, rights, units, ep):
    n, rows, half = len(rights), *rights[0].shape
    total = n * rows
    shapes = [jax.ShapeDtypeStruct((total, 2 * half), BF16)]
    shapes += [jax.ShapeDtypeStruct((total, units), F32)] * CORES + [jax.ShapeDtypeStruct((8, 128), F32)]
    return pl.pallas_call(
        functools.partial(gather_kernel, n, ep, order),
        in_specs=[SMEM] + [VMEM] * (2 * n),
        out_specs=[VMEM] * len(shapes),
        out_shape=shapes,
        cost_estimate=pl.CostEstimate(flops=total * half, bytes_accessed=8 * total * half, transcendentals=0),
        compiler_params=pltpu.CompilerParams(vmem_limit_bytes=16 << 20),
    )(place, *lefts, *rights)


def preload_kernel(n, *refs):
    sems = refs[2 * n]
    copies = [pltpu.make_async_copy(refs[i], refs[n + i], sems.at[i]) for i in range(n)]
    for c in copies:
        c.start()
    for c in copies:
        c.wait()


def preload(weights):
    n = len(weights)
    size = sum(w.size for w in weights)
    return pl.pallas_call(
        functools.partial(preload_kernel, n),
        in_specs=[HBM] * n,
        out_specs=[VMEM] * n,
        out_shape=[jax.ShapeDtypeStruct(w.shape, w.dtype) for w in weights],
        scratch_shapes=[pltpu.SemaphoreType.DMA((n,))],
        cost_estimate=pl.CostEstimate(flops=size, bytes_accessed=4 * size, transcendentals=0),
        compiler_params=pltpu.CompilerParams(vmem_limit_bytes=14 << 20),
    )(*weights)


def down_kernel(n, order, place, *refs):
    before, gates, ups, weights = (refs[i * n:(i + 1) * n] for i in range(4))
    outs = refs[4 * n:-1]
    hid = refs[-1]
    tp = len(order)
    width = outs[0].shape[1]
    size = outs[0].shape[0]

    for w in range(n):
        g = before[w][...]
        hid[w] = (g / (1.0 + jnp.exp(-g)) * ups[w][...] * gates[w][...]).astype(BF16)
    for k in reversed(range(tp)):
        total = None
        cols = pl.ds(pl.multiple_of(lax.rem(place[0] + order[k] % tp, tp) * width, 128), width)
        for w in range(n):
            term = jnp.dot(hid[w], weights[w][0, :, cols], preferred_element_type=F32)
            total = term if total is None else total + term
        total = total.astype(BF16)
        for c in range(CHAINS):
            got = total[c * size:(c + 1) * size]
            if k < tp - 1:
                outs[c * (tp + 1) + k][...] = got
            else:
                outs[c * (tp + 1) + k][...] = got[:size // 2]
                outs[c * (tp + 1) + k + 1][...] = got[size // 2:]


def down(place, order, before, gates, ups, weights):
    total, units = before[0].shape
    tp = len(order)
    depth = weights[0].shape[2]
    width = depth // tp
    size = total // CHAINS
    heights = ([size] * (tp - 1) + [size // 2] * 2) * CHAINS
    n = len(before)
    outs = pl.pallas_call(
        functools.partial(down_kernel, n, order),
        in_specs=[SMEM] + [VMEM] * (4 * n),
        out_specs=[VMEM] * len(heights),
        out_shape=[jax.ShapeDtypeStruct((h, width), BF16) for h in heights],
        scratch_shapes=[pltpu.VMEM((n, total, units), BF16)],
        cost_estimate=pl.CostEstimate(
            flops=2 * n * total * depth * units, bytes_accessed=2 * n * depth * units, transcendentals=0
        ),
        compiler_params=pltpu.CompilerParams(vmem_limit_bytes=20 << 20),
    )(place, *before, *gates, *ups, *weights)
    return [outs[c * (tp + 1):(c + 1) * (tp + 1)] for c in range(CHAINS)]


def added(*terms):
    total = terms[0].astype(F32)
    for t in terms[1:]:
        total = total + t.astype(F32)
    return total.astype(BF16)


def shift(a, axis, s):
    n = lax.axis_size(axis)
    return lax.ppermute(a, axis, [(i, (i + s) % n) for i in range(n)])


def hop(a, b, plus, minus):
    h = plus.shape[0]
    if h < a.shape[0]:
        plus = jnp.concatenate([added(a[:h], plus), a[h:]])
        minus = jnp.concatenate([b[:h], added(b[h:], minus)])
    else:
        plus, minus = added(a, plus), added(b, minus)
    return shift(plus, "tp", 1), shift(minus, "tp", -1)


def planned(tokens, w_gate, w_up, w_down, router_logits, expert_ids, draft_lengths, accept_mask):
    rows, depth = tokens.shape
    ring, tp = lax.axis_size("x"), lax.axis_size("tp")
    ep = ring * CORES
    half = depth // 2
    own, core = lax.axis_index("x"), lax.axis_index("core")
    order = [0, 1, -1, 2, -2, 3, -3, 4]
    place = jnp.stack([CORES * own + core, CORES * own + 1 - core, own]).astype(jnp.int32)

    def other(a):
        return shift(a, "core", 1)

    opened = shift(tokens[:, half:], "x", 1)
    left = payload(ep, tokens[:, :half], router_logits, expert_ids, draft_lengths, accept_mask)
    lefts, rights = {0: left}, {0: tokens[:, half:]}
    for k in range(1, ring // 2):
        rights[-k] = opened if k == 1 else shift(rights[1 - k], "x", 1)
        lefts[-k] = shift(lefts[1 - k], "x", 1)
        rights[k] = shift(rights[k - 1], "x", -1)
        lefts[k] = shift(lefts[k - 1], "x", -1)
    far = ring // 2
    sides = [(w_gate, w_up, w_down), tuple(other(w) for w in (w_gate, w_up, w_down))]
    lefts[1 - far], rights[far - 1], *theirs = lax.optimization_barrier((lefts[1 - far], rights[far - 1], *sides[1]))
    lefts[far] = shift(lefts[1 - far], "x", 1)
    rights[far] = shift(rights[far - 1], "x", -1)
    sides[1] = preload(theirs)

    x, *gates, count = gather(place, order, [lefts[k] for k in order], [rights[k] for k in order], w_gate.shape[2], ep)
    mine = count[:1, 0].astype(jnp.int32)
    theirs = other(mine)
    accepted = mine + theirs
    before, ups = ([jnp.dot(x, w[i][0], preferred_element_type=F32) for w in sides] for i in range(2))
    chains = down(lax.axis_index("tp").reshape(1), order, before, gates, ups, [w[2] for w in sides])
    width = depth // tp

    state = [(shift(c[7], "tp", 1), shift(c[8], "tp", -1)) for c in chains]
    for k in (3, 2, 1):
        state = [hop(c[2 * k - 1], c[2 * k], *s) for c, s in zip(chains, state)]
    summed = jnp.concatenate([added(c[0], *s) for c, s in zip(chains, state)])
    parts = lax.all_to_all(summed.reshape(ring, rows, width), "x", split_axis=0, concat_axis=0, tiled=True)
    mixed = jnp.sum(parts.astype(F32), axis=0).astype(BF16)
    return mixed, accepted


def solution(mesh):
    groups, ep, tp = (mesh.shape[a] for a in ("groups", "ep", "tp"))
    planes = Mesh(mesh.devices.reshape(groups, ep // CORES, CORES, tp), ("groups", "x", "core", "tp"))
    split = ("x", "core")
    rows = ("groups", *split)
    placed = (
        P(rows, None),
        P(split, None, "tp"),
        P(split, None, "tp"),
        P(split, "tp", None),
        P(rows, None),
        P(rows, None),
        P(rows),
        P(rows, None),
    )
    return jax.shard_map(
        planned,
        mesh=planes,
        in_specs=placed,
        out_specs=(P(rows, "tp"), P("groups")),
        check_vma=False,
    )
```

profile of v0, /device:TPU:514, one launch (start us, length us, event | category | flops | bytes accessed | tf_op | source)
XLA Modules:
  0.0 145.3 jit_solution(2457940716784883263)
XLA Ops:
  1.4 1.1 fusion.8
  2.5 1.7 %collective-permute-start.13 = (bf16[32,3584]{1,0:T(8,128)(2,1)S(1)}, bf16[32,3584]{1,0:T(8,128)(2,1)S(1)}, u32[]{:S(2)}, u32[]{:S(2)}) collective-permute-start(bf16[32,3584]{1,0:T(8,128)(2,1)S(1)} %get-tuple-element.62.refs_8_), channel_id=1, source_target_pairs={{0,16},{16,32},{32,48},{48,64},{64,80},{80,96},{96,112},{112,0},{1... | collective-permute-start | bytes 688136 | tf_op jit(solution)/shard_map/ppermute | solution.py:176
  4.2 17.9 %collective-permute-start.6 = (bf16[32,3584]{1,0:T(8,128)(2,1)S(1)}, bf16[32,3584]{1,0:T(8,128)(2,1)S(1)}, u32[]{:S(2)}, u32[]{:S(2)}) collective-permute-start(bf16[32,3584]{1,0:T(8,128)(2,1)S(1)} %get-tuple-element.62.refs_8_), channel_id=1, source_target_pairs={{0,112},{16,0},{32,16},{48,32},{64,48},{80,64},{96,80},{112,96},{1... | collective-permute-start | bytes 688136 | tf_op jit(solution)/shard_map/ppermute | solution.py:176
  22.1 0.8 copy.10.logits
  22.9 0.8 copy.11.ids
  25.0 0.8 shard_map.95.refs_0_
  25.8 2.3 %collective-permute-done.13.refs_10_ = bf16[32,3584]{1,0:T(8,128)(2,1)S(1)} collective-permute-done((bf16[32,3584]{1,0:T(8,128)(2,1)S(1)}, bf16[32,3584]{1,0:T(8,128)(2,1)S(1)}, u32[]{:S(2)}, u32[]{:S(2)}) %collective-permute-start.13) | collective-permute-done | bytes 229408 | tf_op jit(solution)/shard_map/ppermute | solution.py:176
  28.1 2.9 %collective-permute-start = (bf16[32,3712]{1,0:T(8,128)(2,1)S(1)}, bf16[32,3712]{1,0:T(8,128)(2,1)S(1)}, u32[]{:S(2)}, u32[]{:S(2)}) collective-permute-start(bf16[32,3712]{1,0:T(8,128)(2,1)S(1)} %shard_map.95.refs_0_), channel_id=1, source_target_pairs={{0,112},{16,0},{32,16},{48,32},{64,48},{80,64},{96,80},{112,96},{1... | collective-permute-start | bytes 712712 | tf_op jit(solution)/shard_map/ppermute | solution.py:176
  31.1 5.4 %collective-permute-done.1.refs_2_ = bf16[32,3712]{1,0:T(8,128)(2,1)S(1)} collective-permute-done((bf16[32,3712]{1,0:T(8,128)(2,1)S(1)}, bf16[32,3712]{1,0:T(8,128)(2,1)S(1)}, u32[]{:S(2)}, u32[]{:S(2)}) %collective-permute-start.1) | collective-permute-done | bytes 237600 | tf_op jit(solution)/shard_map/ppermute | solution.py:176
  36.5 3.0 %collective-permute-start.7 = (bf16[32,3584]{1,0:T(8,128)(2,1)S(1)}, bf16[32,3584]{1,0:T(8,128)(2,1)S(1)}, u32[]{:S(2)}, u32[]{:S(2)}) collective-permute-start(bf16[32,3584]{1,0:T(8,128)(2,1)S(1)} %collective-permute-done.6.refs_9_), channel_id=1, source_target_pairs={{0,112},{16,0},{32,16},{48,32},{64,48},{80,64},{96,80},{112,96},{1... | collective-permute-start | bytes 688136 | tf_op jit(solution)/shard_map/ppermute | solution.py:176
  39.5 3.7 %collective-permute-done.7.refs_11_ = bf16[32,3584]{1,0:T(8,128)(2,1)S(1)} collective-permute-done((bf16[32,3584]{1,0:T(8,128)(2,1)S(1)}, bf16[32,3584]{1,0:T(8,128)(2,1)S(1)}, u32[]{:S(2)}, u32[]{:S(2)}) %collective-permute-start.7) | collective-permute-done | bytes 229408 | tf_op jit(solution)/shard_map/ppermute | solution.py:176
  43.1 2.5 %collective-permute-start.2 = (bf16[32,3712]{1,0:T(8,128)(2,1)S(1)}, bf16[32,3712]{1,0:T(8,128)(2,1)S(1)}, u32[]{:S(2)}, u32[]{:S(2)}) collective-permute-start(bf16[32,3712]{1,0:T(8,128)(2,1)S(1)} %collective-permute-done.refs_1_), channel_id=1, source_target_pairs={{0,112},{16,0},{32,16},{48,32},{64,48},{80,64},{96,80},{112,96},{1... | collective-permute-start | bytes 712712 | tf_op jit(solution)/shard_map/ppermute | solution.py:176
  45.6 1.7 %collective-permute-start.8 = (bf16[32,3584]{1,0:T(8,128)(2,1)S(1)}, bf16[32,3584]{1,0:T(8,128)(2,1)S(1)}, u32[]{:S(2)}, u32[]{:S(2)}) collective-permute-start(bf16[32,3584]{1,0:T(8,128)(2,1)S(1)} %collective-permute-done.7.refs_11_), channel_id=1, source_target_pairs={{0,112},{16,0},{32,16},{48,32},{64,48},{80,64},{96,80},{112,96},{1... | collective-permute-start | bytes 688136 | tf_op jit(solution)/shard_map/ppermute | solution.py:176
  47.3 3.8 %collective-permute-done.2.refs_3_ = bf16[32,3712]{1,0:T(8,128)(2,1)S(1)} collective-permute-done((bf16[32,3712]{1,0:T(8,128)(2,1)S(1)}, bf16[32,3712]{1,0:T(8,128)(2,1)S(1)}, u32[]{:S(2)}, u32[]{:S(2)}) %collective-permute-start.2) | collective-permute-done | bytes 237600 | tf_op jit(solution)/shard_map/ppermute | solution.py:176
  51.2 2.5 %collective-permute-done.8.refs_13_ = bf16[32,3584]{1,0:T(8,128)(2,1)S(1)} collective-permute-done((bf16[32,3584]{1,0:T(8,128)(2,1)S(1)}, bf16[32,3584]{1,0:T(8,128)(2,1)S(1)}, u32[]{:S(2)}, u32[]{:S(2)}) %collective-permute-start.8) | collective-permute-done | bytes 229408 | tf_op jit(solution)/shard_map/ppermute | solution.py:176
  53.6 6.6 %collective-permute-done.5.refs_6_ = bf16[32,3712]{1,0:T(8,128)(2,1)S(1)} collective-permute-done((bf16[32,3712]{1,0:T(8,128)(2,1)S(1)}, bf16[32,3712]{1,0:T(8,128)(2,1)S(1)}, u32[]{:S(2)}, u32[]{:S(2)}) %collective-permute-start.5) | collective-permute-done | bytes 237600 | tf_op jit(solution)/shard_map/ppermute | solution.py:176
  60.2 3.4 %collective-permute-start.4 = (bf16[32,3712]{1,0:T(8,128)(2,1)S(1)}, bf16[32,3712]{1,0:T(8,128)(2,1)S(1)}, u32[]{:S(2)}, u32[]{:S(2)}) collective-permute-start(bf16[32,3712]{1,0:T(8,128)(2,1)S(1)} %collective-permute-done.2.refs_3_), channel_id=1, source_target_pairs={{0,112},{16,0},{32,16},{48,32},{64,48},{80,64},{96,80},{112,96},{1... | collective-permute-start | bytes 712712 | tf_op jit(solution)/shard_map/ppermute | solution.py:176
  63.8 1.3 collective-permute-done.14.refs_12_
  65.1 3.4 %collective-permute-start.16 = (bf16[32,3584]{1,0:T(8,128)(2,1)S(1)}, bf16[32,3584]{1,0:T(8,128)(2,1)}, u32[]{:S(2)}, u32[]{:S(2)}) collective-permute-start(bf16[32,3584]{1,0:T(8,128)(2,1)S(1)} %collective-permute-done.8.refs_13_), channel_id=1, source_target_pairs={{0,112},{16,0},{32,16},{48,32},{64,48},{80,64},{96,80},{112,96},{1... | collective-permute-start | bytes 688136 | tf_op jit(solution)/shard_map/ppermute | solution.py:176
  68.6 4.2 %shard_map.97 = (bf16[1,7168,256]{2,1,0:T(8,128)(2,1)S(1)}, bf16[1,7168,256]{2,1,0:T(8,128)(2,1)S(1)}, bf16[1,256,7168]{2,1,0:T(8,128)(2,1)S(1)}) custom-call(bf16[1,7168,256]{2,1,0:T(8,128)(2,1)} %collective-permute-done.9.refs_0_, bf16[1,7168,256]{2,1,0:T(8,128)(2,1)} %collective-permute-done.10.refs_1_, bf16[1,256,7168]{2,1,0:T(8,128)(2,1)} %collective-permute-done.11.refs_2_), custom_call_target="tpu_custom_call" | custom-call | flops 5505024 | bytes 22020096 | tf_op jit(solution)/shard_map/pallas_call | solution.py:107
  72.9 1.4 shard_map.96
  75.0 1.1 fusion.2.refs_4_
  76.1 0.9 copy-done.4
  77.0 1.1 fusion.6.refs_0_
  78.2 1.1 fusion.refs_5_
  79.3 1.1 fusion.4.refs_1_
  80.4 0.9 copy-done
  81.3 2.4 %shard_map.98 = (bf16[128,896]{1,0:T(8,128)(2,1)S(1)}, bf16[128,896]{1,0:T(8,128)(2,1)S(1)}, bf16[128,896]{1,0:T(8,128)(2,1)S(1)}, bf16[128,896]{1,0:T(8,128)(2,...) custom-call(s32[1]{0:T(128)} %bitcast.place, ...), custom_call_target="tpu_custom_call" | custom-call | flops 1879048192 | bytes 7340032 | tf_op jit(solution)/shard_map/pallas_call | solution.py:153
  84.0 2.1 %collective-permute-start.17 = (bf16[64,896]{1,0:T(8,128)(2,1)S(1)}, bf16[64,896]{1,0:T(8,128)(2,1)S(1)}, u32[]{:S(2)}, u32[]{:S(2)}) collective-permute-start(bf16[64,896]{1,0:T(8,128)(2,1)S(1)} %get-tuple-element.47), channel_id=1, source_target_pairs={{0,1},{1,2},{2,3},{3,4},{4,5},{5,6},{6,7},{7,0},{8,9},{9,10},{10,1... | collective-permute-start | bytes 344072 | tf_op jit(solution)/shard_map/ppermute | solution.py:176
  86.1 1.2 collective-permute-start.21
  87.3 0.8 collective-permute-start.25
  88.1 1.2 collective-permute-done.29
  89.4 1.3 collective-permute-start.30
  90.7 3.8 %collective-permute-done.25 = bf16[64,896]{1,0:T(8,128)(2,1)S(1)} collective-permute-done((bf16[64,896]{1,0:T(8,128)(2,1)S(1)}, bf16[64,896]{1,0:T(8,128)(2,1)S(1)}, u32[]{:S(2)}, u32[]{:S(2)}) %collective-permute-start.25) | collective-permute-done | bytes 114720 | tf_op jit(solution)/shard_map/ppermute | solution.py:176
  94.8 3.5 %collective-permute-start.22 = (bf16[128,896]{1,0:T(8,128)(2,1)S(1)}, bf16[128,896]{1,0:T(8,128)(2,1)S(1)}, u32[]{:S(2)}, u32[]{:S(2)}) collective-permute-start(bf16[128,896]{1,0:T(8,128)(2,1)S(1)} %pad_maximum_fusion.2), channel_id=1, source_target_pairs={{0,7},{1,0},{2,1},{3,2},{4,3},{5,4},{6,5},{7,6},{8,15},{9,8},{10,9... | collective-permute-start | bytes 688136 | tf_op jit(solution)/shard_map/ppermute | solution.py:176
  98.6 3.3 %collective-permute-start.31 = (bf16[128,896]{1,0:T(8,128)(2,1)S(1)}, bf16[128,896]{1,0:T(8,128)(2,1)S(1)}, u32[]{:S(2)}, u32[]{:S(2)}) collective-permute-start(bf16[128,896]{1,0:T(8,128)(2,1)S(1)} %add_convert_fusion.2), channel_id=1, source_target_pairs={{0,7},{1,0},{2,1},{3,2},{4,3},{5,4},{6,5},{7,6},{8,15},{9,8},{10,9... | collective-permute-start | bytes 688136 | tf_op jit(solution)/shard_map/ppermute | solution.py:176
  101.9 1.9 %collective-permute-done.26 = bf16[128,896]{1,0:T(8,128)(2,1)S(1)} collective-permute-done((bf16[128,896]{1,0:T(8,128)(2,1)S(1)}, bf16[128,896]{1,0:T(8,128)(2,1)S(1)}, u32[]{:S(2)}, u32[]{:S(2)}) %collective-permute-start.26) | collective-permute-done | bytes 229408 | tf_op jit(solution)/shard_map/ppermute | solution.py:176
  104.1 3.3 %collective-permute-start.23 = (bf16[128,896]{1,0:T(8,128)(2,1)S(1)}, bf16[128,896]{1,0:T(8,128)(2,1)S(1)}, u32[]{:S(2)}, u32[]{:S(2)}) collective-permute-start(bf16[128,896]{1,0:T(8,128)(2,1)S(1)} %add_convert_fusion.7), channel_id=1, source_target_pairs={{0,7},{1,0},{2,1},{3,2},{4,3},{5,4},{6,5},{7,6},{8,15},{9,8},{10,9... | collective-permute-start | bytes 688136 | tf_op jit(solution)/shard_map/ppermute | solution.py:176
  107.4 1.3 collective-permute-done.18
  109.1 3.3 %collective-permute-start.32 = (bf16[128,896]{1,0:T(8,128)(2,1)S(1)}, bf16[128,896]{1,0:T(8,128)(2,1)S(1)}, u32[]{:S(2)}, u32[]{:S(2)}) collective-permute-start(bf16[128,896]{1,0:T(8,128)(2,1)S(1)} %add_convert_fusion.1), channel_id=1, source_target_pairs={{0,7},{1,0},{2,1},{3,2},{4,3},{5,4},{6,5},{7,6},{8,15},{9,8},{10,9... | collective-permute-start | bytes 688136 | tf_op jit(solution)/shard_map/ppermute | solution.py:176
  112.4 1.4 collective-permute-done.27
  114.0 3.3 %collective-permute-start.24 = (bf16[128,896]{1,0:T(8,128)(2,1)S(1)}, bf16[128,896]{1,0:T(8,128)(2,1)S(1)}, u32[]{:S(2)}, u32[]{:S(2)}) collective-permute-start(bf16[128,896]{1,0:T(8,128)(2,1)S(1)} %add_convert_fusion.6), channel_id=1, source_target_pairs={{0,7},{1,0},{2,1},{3,2},{4,3},{5,4},{6,5},{7,6},{8,15},{9,8},{10,9... | collective-permute-start | bytes 688136 | tf_op jit(solution)/shard_map/ppermute | solution.py:176
  117.5 3.6 %collective-permute-done.28 = bf16[128,896]{1,0:T(8,128)(2,1)S(1)} collective-permute-done((bf16[128,896]{1,0:T(8,128)(2,1)S(1)}, bf16[128,896]{1,0:T(8,128)(2,1)S(1)}, u32[]{:S(2)}, u32[]{:S(2)}) %collective-permute-start.28) | collective-permute-done | bytes 229408 | tf_op jit(solution)/shard_map/ppermute | solution.py:176
  121.2 3.5 %collective-permute-done.20 = bf16[128,896]{1,0:T(8,128)(2,1)S(1)} collective-permute-done((bf16[128,896]{1,0:T(8,128)(2,1)S(1)}, bf16[128,896]{1,0:T(8,128)(2,1)S(1)}, u32[]{:S(2)}, u32[]{:S(2)}) %collective-permute-start.20) | collective-permute-done | bytes 229408 | tf_op jit(solution)/shard_map/ppermute | solution.py:176
  124.8 0.8 pad_maximum_fusion
  125.6 6.7 %all-to-all-start = ((bf16[8,32,896]{2,1,0:T(8,128)(2,1)}), bf16[8,32,896]{2,1,0:T(8,128)(2,1)S(1)}, u32[]{:S(2)}, u32[]{:S(2)}) async-start(bf16[8,32,896]{2,1,0:T(8,128)(2,1)} %bitcast.8), calls=%async_computation | async-start | bytes 917504 | tf_op jit(solution)/shard_map/all_to_all | solution.py:228
  133.5 1.1 collective-permute-start.33
  135.5 8.0 %all-to-all-done = bf16[8,32,896]{2,1,0:T(8,128)(2,1)S(1)} async-done(((bf16[8,32,896]{2,1,0:T(8,128)(2,1)}), bf16[8,32,896]{2,1,0:T(8,128)(2,1)S(1)}, u32[]{:S(2)}, u32[]{:S(2)}) %all-to-all-start) | async-done | bytes 458784 | tf_op jit(solution)/shard_map/all_to_all | solution.py:228
  (69 shorter events, 6.4 us)
Async XLA Ops:
  0.6 63.0 %collective-permute-start.9 = (bf16[1,7168,256]{2,1,0:T(8,128)(2,1)}, bf16[1,7168,256]{2,1,0:T(8,128)(2,1)}, u32[]{:S(2)}, u32[]{:S(2)}) collective-permute-start(bf16[1,7168,256]{2,1,0:T(8,128)(2,1)} %param.9), channel_id=1, source_target_pairs={{0,8},{8,0},{1,9},{9,1},{2,10},{10,2},{3,11},{11,3},{4,12},{12,4},... | collective-permute-start | bytes 11010056 | tf_op jit(solution)/shard_map/ppermute | solution.py:176
  0.8 62.8 %collective-permute-start.10 = (bf16[1,7168,256]{2,1,0:T(8,128)(2,1)}, bf16[1,7168,256]{2,1,0:T(8,128)(2,1)}, u32[]{:S(2)}, u32[]{:S(2)}) collective-permute-start(bf16[1,7168,256]{2,1,0:T(8,128)(2,1)} %param.10), channel_id=1, source_target_pairs={{0,8},{8,0},{1,9},{9,1},{2,10},{10,2},{3,11},{11,3},{4,12},{12,4},... | collective-permute-start | bytes 11010056 | tf_op jit(solution)/shard_map/ppermute | solution.py:176
  1.3 62.4 %collective-permute-start.11 = (bf16[1,256,7168]{2,1,0:T(8,128)(2,1)}, bf16[1,256,7168]{2,1,0:T(8,128)(2,1)}, u32[]{:S(2)}, u32[]{:S(2)}) collective-permute-start(bf16[1,256,7168]{2,1,0:T(8,128)(2,1)} %refs_6_.1), channel_id=1, source_target_pairs={{0,8},{8,0},{1,9},{9,1},{2,10},{10,2},{3,11},{11,3},{4,12},{12,4},... | collective-permute-start | bytes 11010056 | tf_op jit(solution)/shard_map/ppermute | solution.py:176
  2.5 25.6 %collective-permute-start.13 = (bf16[32,3584]{1,0:T(8,128)(2,1)S(1)}, bf16[32,3584]{1,0:T(8,128)(2,1)S(1)}, u32[]{:S(2)}, u32[]{:S(2)}) collective-permute-start(bf16[32,3584]{1,0:T(8,128)(2,1)S(1)} %get-tuple-element.62.refs_8_), channel_id=1, source_target_pairs={{0,16},{16,32},{32,48},{48,64},{64,80},{80,96},{96,112},{112,0},{1... | collective-permute-start | bytes 688136 | tf_op jit(solution)/shard_map/ppermute | solution.py:176
  4.2 23.9 %collective-permute-start.6 = (bf16[32,3584]{1,0:T(8,128)(2,1)S(1)}, bf16[32,3584]{1,0:T(8,128)(2,1)S(1)}, u32[]{:S(2)}, u32[]{:S(2)}) collective-permute-start(bf16[32,3584]{1,0:T(8,128)(2,1)S(1)} %get-tuple-element.62.refs_8_), channel_id=1, source_target_pairs={{0,112},{16,0},{32,16},{48,32},{64,48},{80,64},{96,80},{112,96},{1... | collective-permute-start | bytes 688136 | tf_op jit(solution)/shard_map/ppermute | solution.py:176
  23.7 0.7 copy-start.1
  24.3 0.7 copy-start.2
  28.1 8.4 %collective-permute-start.1 = (bf16[32,3712]{1,0:T(8,128)(2,1)S(1)}, bf16[32,3712]{1,0:T(8,128)(2,1)S(1)}, u32[]{:S(2)}, u32[]{:S(2)}) collective-permute-start(bf16[32,3712]{1,0:T(8,128)(2,1)S(1)} %shard_map.95.refs_0_), channel_id=1, source_target_pairs={{0,16},{16,32},{32,48},{48,64},{64,80},{80,96},{96,112},{112,0},{1... | collective-permute-start | bytes 712712 | tf_op jit(solution)/shard_map/ppermute | solution.py:176
  28.1 11.3 %collective-permute-start = (bf16[32,3712]{1,0:T(8,128)(2,1)S(1)}, bf16[32,3712]{1,0:T(8,128)(2,1)S(1)}, u32[]{:S(2)}, u32[]{:S(2)}) collective-permute-start(bf16[32,3712]{1,0:T(8,128)(2,1)S(1)} %shard_map.95.refs_0_), channel_id=1, source_target_pairs={{0,112},{16,0},{32,16},{48,32},{64,48},{80,64},{96,80},{112,96},{1... | collective-permute-start | bytes 712712 | tf_op jit(solution)/shard_map/ppermute | solution.py:176
  36.5 6.6 %collective-permute-start.7 = (bf16[32,3584]{1,0:T(8,128)(2,1)S(1)}, bf16[32,3584]{1,0:T(8,128)(2,1)S(1)}, u32[]{:S(2)}, u32[]{:S(2)}) collective-permute-start(bf16[32,3584]{1,0:T(8,128)(2,1)S(1)} %collective-permute-done.6.refs_9_), channel_id=1, source_target_pairs={{0,112},{16,0},{32,16},{48,32},{64,48},{80,64},{96,80},{112,96},{1... | collective-permute-start | bytes 688136 | tf_op jit(solution)/shard_map/ppermute | solution.py:176
  39.5 6.2 %collective-permute-start.3 = (bf16[32,3712]{1,0:T(8,128)(2,1)S(1)}, bf16[32,3712]{1,0:T(8,128)(2,1)S(1)}, u32[]{:S(2)}, u32[]{:S(2)}) collective-permute-start(bf16[32,3712]{1,0:T(8,128)(2,1)S(1)} %collective-permute-done.1.refs_2_), channel_id=1, source_target_pairs={{0,16},{16,32},{32,48},{48,64},{64,80},{80,96},{96,112},{112,0},{1... | collective-permute-start | bytes 712712 | tf_op jit(solution)/shard_map/ppermute | solution.py:176
  43.1 8.0 %collective-permute-start.2 = (bf16[32,3712]{1,0:T(8,128)(2,1)S(1)}, bf16[32,3712]{1,0:T(8,128)(2,1)S(1)}, u32[]{:S(2)}, u32[]{:S(2)}) collective-permute-start(bf16[32,3712]{1,0:T(8,128)(2,1)S(1)} %collective-permute-done.refs_1_), channel_id=1, source_target_pairs={{0,112},{16,0},{32,16},{48,32},{64,48},{80,64},{96,80},{112,96},{1... | collective-permute-start | bytes 712712 | tf_op jit(solution)/shard_map/ppermute | solution.py:176
  45.6 8.0 %collective-permute-start.8 = (bf16[32,3584]{1,0:T(8,128)(2,1)S(1)}, bf16[32,3584]{1,0:T(8,128)(2,1)S(1)}, u32[]{:S(2)}, u32[]{:S(2)}) collective-permute-start(bf16[32,3584]{1,0:T(8,128)(2,1)S(1)} %collective-permute-done.7.refs_11_), channel_id=1, source_target_pairs={{0,112},{16,0},{32,16},{48,32},{64,48},{80,64},{96,80},{112,96},{1... | collective-permute-start | bytes 688136 | tf_op jit(solution)/shard_map/ppermute | solution.py:176
  51.2 9.0 %collective-permute-start.5 = (bf16[32,3712]{1,0:T(8,128)(2,1)S(1)}, bf16[32,3712]{1,0:T(8,128)(2,1)S(1)}, u32[]{:S(2)}, u32[]{:S(2)}) collective-permute-start(bf16[32,3712]{1,0:T(8,128)(2,1)S(1)} %collective-permute-done.3.refs_4_), channel_id=1, source_target_pairs={{0,16},{16,32},{32,48},{48,64},{64,80},{80,96},{96,112},{112,0},{1... | collective-permute-start | bytes 712712 | tf_op jit(solution)/shard_map/ppermute | solution.py:176
  53.6 11.5 %collective-permute-start.14 = (bf16[32,3584]{1,0:T(8,128)(2,1)S(1)}, bf16[32,3584]{1,0:T(8,128)(2,1)S(1)}, u32[]{:S(2)}, u32[]{:S(2)}) collective-permute-start(bf16[32,3584]{1,0:T(8,128)(2,1)S(1)} %collective-permute-done.13.refs_10_), channel_id=1, source_target_pairs={{0,16},{16,32},{32,48},{48,64},{64,80},{80,96},{96,112},{112,0},{1... | collective-permute-start | bytes 688136 | tf_op jit(solution)/shard_map/ppermute | solution.py:176
  60.2 12.7 %collective-permute-start.4 = (bf16[32,3712]{1,0:T(8,128)(2,1)S(1)}, bf16[32,3712]{1,0:T(8,128)(2,1)S(1)}, u32[]{:S(2)}, u32[]{:S(2)}) collective-permute-start(bf16[32,3712]{1,0:T(8,128)(2,1)S(1)} %collective-permute-done.2.refs_3_), channel_id=1, source_target_pairs={{0,112},{16,0},{32,16},{48,32},{64,48},{80,64},{96,80},{112,96},{1... | collective-permute-start | bytes 712712 | tf_op jit(solution)/shard_map/ppermute | solution.py:176
  63.6 9.3 %collective-permute-start.12 = (bf16[32,3712]{1,0:T(8,128)(2,1)S(1)}, bf16[32,3712]{1,0:T(8,128)(2,1)S(1)}, u32[]{:S(2)}, u32[]{:S(2)}) collective-permute-start(bf16[32,3712]{1,0:T(8,128)(2,1)S(1)} %collective-permute-done.5.refs_6_), channel_id=1, source_target_pairs={{0,16},{16,32},{32,48},{48,64},{64,80},{80,96},{96,112},{112,0},{1... | collective-permute-start | bytes 712712 | tf_op jit(solution)/shard_map/ppermute | solution.py:176
  65.1 7.8 %collective-permute-start.15 = (bf16[32,3584]{1,0:T(8,128)(2,1)S(1)}, bf16[32,3584]{1,0:T(8,128)(2,1)S(1)}, u32[]{:S(2)}, u32[]{:S(2)}) collective-permute-start(bf16[32,3584]{1,0:T(8,128)(2,1)S(1)} %collective-permute-done.14.refs_12_), channel_id=1, source_target_pairs={{0,16},{16,32},{32,48},{48,64},{64,80},{80,96},{96,112},{112,0},{1... | collective-permute-start | bytes 688136 | tf_op jit(solution)/shard_map/ppermute | solution.py:176
  65.1 7.8 %collective-permute-start.16 = (bf16[32,3584]{1,0:T(8,128)(2,1)S(1)}, bf16[32,3584]{1,0:T(8,128)(2,1)}, u32[]{:S(2)}, u32[]{:S(2)}) collective-permute-start(bf16[32,3584]{1,0:T(8,128)(2,1)S(1)} %collective-permute-done.8.refs_13_), channel_id=1, source_target_pairs={{0,112},{16,0},{32,16},{48,32},{64,48},{80,64},{96,80},{112,96},{1... | collective-permute-start | bytes 688136 | tf_op jit(solution)/shard_map/ppermute | solution.py:176
  72.9 2.2 %copy-start.3 = (bf16[1,7168,256]{2,1,0:T(8,128)(2,1)S(1)}, bf16[1,7168,256]{2,1,0:T(8,128)(2,1)}, u32[]{:S(2)}) copy-start(bf16[1,7168,256]{2,1,0:T(8,128)(2,1)} %param.10) | copy-start | bytes 11010052
  75.0 2.0 %copy-start.4 = (bf16[1,7168,256]{2,1,0:T(8,128)(2,1)S(1)}, bf16[1,7168,256]{2,1,0:T(8,128)(2,1)}, u32[]{:S(2)}) copy-start(bf16[1,7168,256]{2,1,0:T(8,128)(2,1)} %param.9) | copy-start | bytes 11010052
  79.3 2.0 %copy-start = (bf16[1,256,7168]{2,1,0:T(8,128)(2,1)S(1)}, bf16[1,256,7168]{2,1,0:T(8,128)(2,1)}, u32[]{:S(2)}) copy-start(bf16[1,256,7168]{2,1,0:T(8,128)(2,1)} %refs_6_.1) | copy-start | bytes 11010052
  83.7 5.6 %collective-permute-start.29 = (bf16[64,896]{1,0:T(8,128)(2,1)S(1)}, bf16[64,896]{1,0:T(8,128)(2,1)S(1)}, u32[]{:S(2)}, u32[]{:S(2)}) collective-permute-start(bf16[64,896]{1,0:T(8,128)(2,1)S(1)} %get-tuple-element.60), channel_id=1, source_target_pairs={{0,7},{1,0},{2,1},{3,2},{4,3},{5,4},{6,5},{7,6},{8,15},{9,8},{10,9... | collective-permute-start | bytes 344072 | tf_op jit(solution)/shard_map/ppermute | solution.py:176
  84.0 14.4 %collective-permute-start.17 = (bf16[64,896]{1,0:T(8,128)(2,1)S(1)}, bf16[64,896]{1,0:T(8,128)(2,1)S(1)}, u32[]{:S(2)}, u32[]{:S(2)}) collective-permute-start(bf16[64,896]{1,0:T(8,128)(2,1)S(1)} %get-tuple-element.47), channel_id=1, source_target_pairs={{0,1},{1,2},{2,3},{3,4},{4,5},{5,6},{6,7},{7,0},{8,9},{9,10},{10,1... | collective-permute-start | bytes 344072 | tf_op jit(solution)/shard_map/ppermute | solution.py:176
  86.1 8.7 %collective-permute-start.21 = (bf16[64,896]{1,0:T(8,128)(2,1)S(1)}, bf16[64,896]{1,0:T(8,128)(2,1)S(1)}, u32[]{:S(2)}, u32[]{:S(2)}) collective-permute-start(bf16[64,896]{1,0:T(8,128)(2,1)S(1)} %get-tuple-element.51), channel_id=1, source_target_pairs={{0,7},{1,0},{2,1},{3,2},{4,3},{5,4},{6,5},{7,6},{8,15},{9,8},{10,9... | collective-permute-start | bytes 344072 | tf_op jit(solution)/shard_map/ppermute | solution.py:176
  87.3 7.2 %collective-permute-start.25 = (bf16[64,896]{1,0:T(8,128)(2,1)S(1)}, bf16[64,896]{1,0:T(8,128)(2,1)S(1)}, u32[]{:S(2)}, u32[]{:S(2)}) collective-permute-start(bf16[64,896]{1,0:T(8,128)(2,1)S(1)} %get-tuple-element.56), channel_id=1, source_target_pairs={{0,1},{1,2},{2,3},{3,4},{4,5},{5,6},{6,7},{7,0},{8,9},{9,10},{10,1... | collective-permute-start | bytes 344072 | tf_op jit(solution)/shard_map/ppermute | solution.py:176
  89.4 9.2 %collective-permute-start.30 = (bf16[128,896]{1,0:T(8,128)(2,1)S(1)}, bf16[128,896]{1,0:T(8,128)(2,1)S(1)}, u32[]{:S(2)}, u32[]{:S(2)}) collective-permute-start(bf16[128,896]{1,0:T(8,128)(2,1)S(1)} %pad_maximum_fusion.4), channel_id=1, source_target_pairs={{0,7},{1,0},{2,1},{3,2},{4,3},{5,4},{6,5},{7,6},{8,15},{9,8},{10,9... | collective-permute-start | bytes 688136 | tf_op jit(solution)/shard_map/ppermute | solution.py:176
  94.6 9.3 %collective-permute-start.26 = (bf16[128,896]{1,0:T(8,128)(2,1)S(1)}, bf16[128,896]{1,0:T(8,128)(2,1)S(1)}, u32[]{:S(2)}, u32[]{:S(2)}) collective-permute-start(bf16[128,896]{1,0:T(8,128)(2,1)S(1)} %pad_maximum_fusion.3), channel_id=1, source_target_pairs={{0,1},{1,2},{2,3},{3,4},{4,5},{5,6},{6,7},{7,0},{8,9},{9,10},{10,1... | collective-permute-start | bytes 688136 | tf_op jit(solution)/shard_map/ppermute | solution.py:176
  94.8 9.2 %collective-permute-start.22 = (bf16[128,896]{1,0:T(8,128)(2,1)S(1)}, bf16[128,896]{1,0:T(8,128)(2,1)S(1)}, u32[]{:S(2)}, u32[]{:S(2)}) collective-permute-start(bf16[128,896]{1,0:T(8,128)(2,1)S(1)} %pad_maximum_fusion.2), channel_id=1, source_target_pairs={{0,7},{1,0},{2,1},{3,2},{4,3},{5,4},{6,5},{7,6},{8,15},{9,8},{10,9... | collective-permute-start | bytes 688136 | tf_op jit(solution)/shard_map/ppermute | solution.py:176
  98.4 10.4 %collective-permute-start.18 = (bf16[128,896]{1,0:T(8,128)(2,1)S(1)}, bf16[128,896]{1,0:T(8,128)(2,1)S(1)}, u32[]{:S(2)}, u32[]{:S(2)}) collective-permute-start(bf16[128,896]{1,0:T(8,128)(2,1)S(1)} %pad_maximum_fusion.1), channel_id=1, source_target_pairs={{0,1},{1,2},{2,3},{3,4},{4,5},{5,6},{6,7},{7,0},{8,9},{9,10},{10,1... | collective-permute-start | bytes 688136 | tf_op jit(solution)/shard_map/ppermute | solution.py:176
  98.6 10.3 %collective-permute-start.31 = (bf16[128,896]{1,0:T(8,128)(2,1)S(1)}, bf16[128,896]{1,0:T(8,128)(2,1)S(1)}, u32[]{:S(2)}, u32[]{:S(2)}) collective-permute-start(bf16[128,896]{1,0:T(8,128)(2,1)S(1)} %add_convert_fusion.2), channel_id=1, source_target_pairs={{0,7},{1,0},{2,1},{3,2},{4,3},{5,4},{6,5},{7,6},{8,15},{9,8},{10,9... | collective-permute-start | bytes 688136 | tf_op jit(solution)/shard_map/ppermute | solution.py:176
  103.9 9.8 %collective-permute-start.27 = (bf16[128,896]{1,0:T(8,128)(2,1)S(1)}, bf16[128,896]{1,0:T(8,128)(2,1)S(1)}, u32[]{:S(2)}, u32[]{:S(2)}) collective-permute-start(bf16[128,896]{1,0:T(8,128)(2,1)S(1)} %add_convert_fusion.4), channel_id=1, source_target_pairs={{0,1},{1,2},{2,3},{3,4},{4,5},{5,6},{6,7},{7,0},{8,9},{9,10},{10,1... | collective-permute-start | bytes 688136 | tf_op jit(solution)/shard_map/ppermute | solution.py:176
  104.1 9.8 %collective-permute-start.23 = (bf16[128,896]{1,0:T(8,128)(2,1)S(1)}, bf16[128,896]{1,0:T(8,128)(2,1)S(1)}, u32[]{:S(2)}, u32[]{:S(2)}) collective-permute-start(bf16[128,896]{1,0:T(8,128)(2,1)S(1)} %add_convert_fusion.7), channel_id=1, source_target_pairs={{0,7},{1,0},{2,1},{3,2},{4,3},{5,4},{6,5},{7,6},{8,15},{9,8},{10,9... | collective-permute-start | bytes 688136 | tf_op jit(solution)/shard_map/ppermute | solution.py:176
  108.8 8.5 %collective-permute-start.19 = (bf16[128,896]{1,0:T(8,128)(2,1)S(1)}, bf16[128,896]{1,0:T(8,128)(2,1)S(1)}, u32[]{:S(2)}, u32[]{:S(2)}) collective-permute-start(bf16[128,896]{1,0:T(8,128)(2,1)S(1)} %add_convert_fusion.9), channel_id=1, source_target_pairs={{0,1},{1,2},{2,3},{3,4},{4,5},{5,6},{6,7},{7,0},{8,9},{9,10},{10,1... | collective-permute-start | bytes 688136 | tf_op jit(solution)/shard_map/ppermute | solution.py:176
  109.1 8.5 %collective-permute-start.32 = (bf16[128,896]{1,0:T(8,128)(2,1)S(1)}, bf16[128,896]{1,0:T(8,128)(2,1)S(1)}, u32[]{:S(2)}, u32[]{:S(2)}) collective-permute-start(bf16[128,896]{1,0:T(8,128)(2,1)S(1)} %add_convert_fusion.1), channel_id=1, source_target_pairs={{0,7},{1,0},{2,1},{3,2},{4,3},{5,4},{6,5},{7,6},{8,15},{9,8},{10,9... | collective-permute-start | bytes 688136 | tf_op jit(solution)/shard_map/ppermute | solution.py:176
  113.8 7.3 %collective-permute-start.28 = (bf16[128,896]{1,0:T(8,128)(2,1)S(1)}, bf16[128,896]{1,0:T(8,128)(2,1)S(1)}, u32[]{:S(2)}, u32[]{:S(2)}) collective-permute-start(bf16[128,896]{1,0:T(8,128)(2,1)S(1)} %add_convert_fusion.3), channel_id=1, source_target_pairs={{0,1},{1,2},{2,3},{3,4},{4,5},{5,6},{6,7},{7,0},{8,9},{9,10},{10,1... | collective-permute-start | bytes 688136 | tf_op jit(solution)/shard_map/ppermute | solution.py:176
  114.0 7.2 %collective-permute-start.24 = (bf16[128,896]{1,0:T(8,128)(2,1)S(1)}, bf16[128,896]{1,0:T(8,128)(2,1)S(1)}, u32[]{:S(2)}, u32[]{:S(2)}) collective-permute-start(bf16[128,896]{1,0:T(8,128)(2,1)S(1)} %add_convert_fusion.6), channel_id=1, source_target_pairs={{0,7},{1,0},{2,1},{3,2},{4,3},{5,4},{6,5},{7,6},{8,15},{9,8},{10,9... | collective-permute-start | bytes 688136 | tf_op jit(solution)/shard_map/ppermute | solution.py:176
  117.4 7.3 %collective-permute-start.20 = (bf16[128,896]{1,0:T(8,128)(2,1)S(1)}, bf16[128,896]{1,0:T(8,128)(2,1)S(1)}, u32[]{:S(2)}, u32[]{:S(2)}) collective-permute-start(bf16[128,896]{1,0:T(8,128)(2,1)S(1)} %add_convert_fusion.8), channel_id=1, source_target_pairs={{0,1},{1,2},{2,3},{3,4},{4,5},{5,6},{6,7},{7,0},{8,9},{9,10},{10,1... | collective-permute-start | bytes 688136 | tf_op jit(solution)/shard_map/ppermute | solution.py:176
  125.6 17.9 %all-to-all-start = ((bf16[8,32,896]{2,1,0:T(8,128)(2,1)}), bf16[8,32,896]{2,1,0:T(8,128)(2,1)S(1)}, u32[]{:S(2)}, u32[]{:S(2)}) async-start(bf16[8,32,896]{2,1,0:T(8,128)(2,1)} %bitcast.8), calls=%async_computation | async-start | bytes 917504 | tf_op jit(solution)/shard_map/all_to_all | solution.py:228
  133.5 1.4 collective-permute-start.33
where the time goes:
time: 146 us; the launch traced here: 145 us
  starting transfers between devices  68.5 us (47%)
  waiting for transfers between devices  50.7 us (35%)
  Pallas kernels  8.84 us (6%)
  local copies, waits for them, and re-layouts  7.02 us (5%)
  matrix products  4.43 us (3%)
  between operations  3.46 us (2%)
  other arithmetic  2.41 us (2%)
    ppermute x34, starting transfers between devices, shift(): return lax.ppermute(a, axis, [(i, (i + s) % n) for i in range(n)])  61.8 us
    ppermute x34, waiting for transfers between devices, shift(): return lax.ppermute(a, axis, [(i, (i + s) % n) for i in range(n)])  42.7 us
    all_to_all x1, waiting for transfers between devices, planned(): lax.all_to_all(summed.reshape(ring, rows, width), 'x', split_axis=0, conc...  7.99 us
    all_to_all x1, starting transfers between devices, planned(): lax.all_to_all(summed.reshape(ring, rows, width), 'x', split_axis=0, conc...  6.7 us
    unnamed x12, local copies, waits for them, and re-layouts  5.38 us
    dot_general x4, matrix products, planned(): jnp.dot(x, w[i][0], preferred_element_type=F32)  4.43 us
    pallas_call x1, Pallas kernels, preload(): pl.pallas_call(functools.partial(preload_kernel, n), in_specs=[HBM] * n,...  4.23 us
  transfers between devices with their start and end apart: 35, of which 16 were waited for; matrix products, arithmetic and copies ran while one was open for 3% of the time, Pallas kernels for 3%

commit v1 on v0

--- a/solution.py
+++ b/solution.py
@@ -20,19 +20,24 @@
 HBM = pl.BlockSpec(memory_space=pltpu.HBM)
 
 
-def payload_kernel(ep, lengths, mask, tokens, logits, ids, left):
+def count_kernel(lengths, mask, total):
+    count = jnp.int32(0)
+    for r in range(mask.shape[0]):
+        prefix = jnp.int32(1)
+        for j in range(DRAFT):
+            prefix = prefix * mask[r, j] * (j < lengths[r]).astype(jnp.int32)
+            count = count + prefix
+    total[0] = count
+
+
+def payload_kernel(ep, lengths, count, tokens, logits, ids, left):
     rows, half = tokens.shape
     top = ids.shape[1]
     left[:, :half] = tokens[...]
     row = lax.broadcasted_iota(jnp.int32, (rows, EXTRA), 0)
     lane = lax.broadcasted_iota(jnp.int32, (rows, EXTRA), 1)
-    count = jnp.int32(0)
     live = jnp.zeros((rows, EXTRA), jnp.int32)
     for r in range(rows // DRAFT):
-        prefix = jnp.int32(1)
-        for j in range(DRAFT):
-            prefix = prefix * mask[r, j] * (j < lengths[r]).astype(jnp.int32)
-            count = count + prefix
         live = live + ((row >= r * DRAFT) & (row < r * DRAFT + lengths[r])).astype(jnp.int32)
     sig = 1.0 / (1.0 + jnp.exp(-logits[...]))
     gates = 2.827 * sig / jnp.sum(sig, axis=1, keepdims=True)
@@ -42,11 +47,11 @@
     dense = jnp.where(live > 0, dense, 0.0)
     high = dense.astype(BF16).astype(F32)
     extra = jnp.where(lane < ep, high, jnp.where(lane < 2 * ep, dense - high, 0.0))
-    extra = jnp.where((lane == 2 * ep) & (row == 0), count.astype(F32), extra)
+    extra = jnp.where((lane == 2 * ep) & (row == 0), count[0].astype(F32), extra)
     left[:, half:] = extra.astype(BF16)
 
 
-def payload(ep, tokens, logits, ids, lengths, mask):
+def payload(ep, tokens, logits, ids, lengths, count):
     rows, half = tokens.shape
     return pl.pallas_call(
         functools.partial(payload_kernel, ep),
@@ -54,7 +59,7 @@
         out_specs=VMEM,
         out_shape=jax.ShapeDtypeStruct((rows, half + EXTRA), BF16),
         compiler_params=pltpu.CompilerParams(vmem_limit_bytes=8 << 20),
-    )(lengths, mask, tokens, logits, ids)
+    )(lengths, count, tokens, logits, ids)
 
 
 def gather_kernel(n, ep, order, place, *refs):
@@ -198,31 +203,35 @@
     def other(a):
         return shift(a, "core", 1)
 
+    mine = pl.pallas_call(
+        count_kernel, in_specs=[SMEM, SMEM], out_specs=SMEM, out_shape=jax.ShapeDtypeStruct((1,), jnp.int32)
+    )(draft_lengths, accept_mask)
+    theirs = other(mine)
+    sides = [(w_gate, w_up, w_down), tuple(other(w) for w in (w_gate, w_up, w_down))]
     opened = shift(tokens[:, half:], "x", 1)
-    left = payload(ep, tokens[:, :half], router_logits, expert_ids, draft_lengths, accept_mask)
+    mirrored = shift(tokens[:, half:], "x", -1)
+    left = payload(ep, tokens[:, :half], router_logits, expert_ids, draft_lengths, mine + theirs)
     lefts, rights = {0: left}, {0: tokens[:, half:]}
     for k in range(1, ring // 2):
         rights[-k] = opened if k == 1 else shift(rights[1 - k], "x", 1)
         lefts[-k] = shift(lefts[1 - k], "x", 1)
-        rights[k] = shift(rights[k - 1], "x", -1)
+        rights[k] = mirrored if k == 1 else shift(rights[k - 1], "x", -1)
         lefts[k] = shift(lefts[k - 1], "x", -1)
     far = ring // 2
-    sides = [(w_gate, w_up, w_down), tuple(other(w) for w in (w_gate, w_up, w_down))]
     lefts[1 - far], rights[far - 1], *theirs = lax.optimization_barrier((lefts[1 - far], rights[far - 1], *sides[1]))
     lefts[far] = shift(lefts[1 - far], "x", 1)
     rights[far] = shift(rights[far - 1], "x", -1)
-    sides[1] = preload(theirs)
+    sides[1] = preload(sides[1])
 
     x, *gates, count = gather(place, order, [lefts[k] for k in order], [rights[k] for k in order], w_gate.shape[2], ep)
-    mine = count[:1, 0].astype(jnp.int32)
-    theirs = other(mine)
-    accepted = mine + theirs
+    accepted = count[:1, 0].astype(jnp.int32)
     before, ups = ([jnp.dot(x, w[i][0], preferred_element_type=F32) for w in sides] for i in range(2))
     chains = down(lax.axis_index("tp").reshape(1), order, before, gates, ups, [w[2] for w in sides])
     width = depth // tp
 
     state = [(shift(c[7], "tp", 1), shift(c[8], "tp", -1)) for c in chains]
-    for k in (3, 2, 1):
+    state = [hop(c[5], c[6], *s) for c, s in zip(chains, state)]
+    for k in (2, 1):
         state = [hop(c[2 * k - 1], c[2 * k], *s) for c, s in zip(chains, state)]
     summed = jnp.concatenate([added(c[0], *s) for c, s in zip(chains, state)])
     parts = lax.all_to_all(summed.reshape(ring, rows, width), "x", split_axis=0, concat_axis=0, tiled=True)

time: 146 us -> 157 us (1.075)
  starting transfers between devices: 68.5 us -> 73.4 us
  waiting for transfers between devices: 50.7 us -> 55.5 us
    ppermute x34, starting transfers between devices: 61.8 us -> 66.5 us  [shift(): return lax.ppermute(a, axis, [(i, (i + s) % n) for i in range(n)])]
    ppermute x34, waiting for transfers between devices: 42.7 us -> 45.6 us  [shift(): return lax.ppermute(a, axis, [(i, (i + s) % n) for i in range(n)])]
    all_to_all x1, waiting for transfers between devices: 7.99 us -> 9.97 us  [planned(): lax.all_to_all(summed.reshape(ring, rows, width), 'x', split_axis=0, conc...]
    unnamed x12 -> x10, local copies, waits for them, and re-layouts: 5.38 us -> 4.7 us
  transfers between devices with their start and end apart: 35 -> 35, of which waited for: 16 -> 15; matrix products, arithmetic and copies ran while one was open for 3% -> 3% of each run, Pallas kernels for 3% -> 4%
where the time goes in v1:
time: 157 us; the launch traced here: 156 us
  starting transfers between devices  73.4 us (47%)
  waiting for transfers between devices  55.5 us (35%)
  Pallas kernels  10.1 us (6%)
  local copies, waits for them, and re-layouts  6.33 us (4%)
  matrix products  4.43 us (3%)
  between operations  4.06 us (3%)
  other arithmetic  2.4 us (2%)
    ppermute x34, starting transfers between devices, shift(): return lax.ppermute(a, axis, [(i, (i + s) % n) for i in range(n)])  66.5 us
    ppermute x34, waiting for transfers between devices, shift(): return lax.ppermute(a, axis, [(i, (i + s) % n) for i in range(n)])  45.6 us
    all_to_all x1, waiting for transfers between devices, planned(): lax.all_to_all(summed.reshape(ring, rows, width), 'x', split_axis=0, conc...  9.97 us
    all_to_all x1, starting transfers between devices, planned(): lax.all_to_all(summed.reshape(ring, rows, width), 'x', split_axis=0, conc...  6.96 us
    unnamed x10, local copies, waits for them, and re-layouts  4.7 us
    dot_general x4, matrix products, planned(): jnp.dot(x, w[i][0], preferred_element_type=F32)  4.43 us
    pallas_call x1, Pallas kernels, preload(): pl.pallas_call(functools.partial(preload_kernel, n), in_specs=[HBM] * n,...  4.23 us
  transfers between devices with their start and end apart: 35, of which 15 were waited for; matrix products, arithmetic and copies ran while one was open for 3% of the time, Pallas kernels for 4%

profile of v1, /device:TPU:514, one launch (start us, length us, event | category | flops | bytes accessed | tf_op | source)
XLA Modules:
  0.0 156.3 jit_solution(5904657365037543111)
XLA Ops:
  1.4 1.1 fusion.8
  2.5 19.5 %collective-permute-start.7 = (bf16[32,3584]{1,0:T(8,128)(2,1)S(1)}, bf16[32,3584]{1,0:T(8,128)(2,1)S(1)}, u32[]{:S(2)}, u32[]{:S(2)}) collective-permute-start(bf16[32,3584]{1,0:T(8,128)(2,1)S(1)} %get-tuple-element.56.refs_8_), channel_id=1, source_target_pairs={{0,112},{16,0},{32,16},{48,32},{64,48},{80,64},{96,80},{112,96},{1... | collective-permute-start | bytes 688136 | tf_op jit(solution)/shard_map/ppermute | solution.py:181
  22.0 1.3 shard_map.95
  23.5 1.3 collective-permute-done
  24.8 0.8 copy.10.logits
  25.6 0.8 copy.11.ids
  27.6 0.6 copy-done.1
  28.2 0.8 shard_map.96.refs_0_
  29.1 14.7 %collective-permute-done.14.refs_10_ = bf16[32,3584]{1,0:T(8,128)(2,1)S(1)} collective-permute-done((bf16[32,3584]{1,0:T(8,128)(2,1)S(1)}, bf16[32,3584]{1,0:T(8,128)(2,1)S(1)}, u32[]{:S(2)}, u32[]{:S(2)}) %collective-permute-start.14) | collective-permute-done | bytes 229408 | tf_op jit(solution)/shard_map/ppermute | solution.py:181
  43.8 3.0 %collective-permute-start.1 = (bf16[32,3712]{1,0:T(8,128)(2,1)S(1)}, bf16[32,3712]{1,0:T(8,128)(2,1)S(1)}, u32[]{:S(2)}, u32[]{:S(2)}) collective-permute-start(bf16[32,3712]{1,0:T(8,128)(2,1)S(1)} %shard_map.96.refs_0_), channel_id=1, source_target_pairs={{0,112},{16,0},{32,16},{48,32},{64,48},{80,64},{96,80},{112,96},{1... | collective-permute-start | bytes 712712 | tf_op jit(solution)/shard_map/ppermute | solution.py:181
  46.9 1.5 collective-permute-done.2.refs_2_
  48.4 3.0 %collective-permute-start.8 = (bf16[32,3584]{1,0:T(8,128)(2,1)S(1)}, bf16[32,3584]{1,0:T(8,128)(2,1)S(1)}, u32[]{:S(2)}, u32[]{:S(2)}) collective-permute-start(bf16[32,3584]{1,0:T(8,128)(2,1)S(1)} %collective-permute-done.7.refs_9_), channel_id=1, source_target_pairs={{0,112},{16,0},{32,16},{48,32},{64,48},{80,64},{96,80},{112,96},{1... | collective-permute-start | bytes 688136 | tf_op jit(solution)/shard_map/ppermute | solution.py:181
  51.3 4.5 %collective-permute-done.8.refs_11_ = bf16[32,3584]{1,0:T(8,128)(2,1)S(1)} collective-permute-done((bf16[32,3584]{1,0:T(8,128)(2,1)S(1)}, bf16[32,3584]{1,0:T(8,128)(2,1)S(1)}, u32[]{:S(2)}, u32[]{:S(2)}) %collective-permute-start.8) | collective-permute-done | bytes 229408 | tf_op jit(solution)/shard_map/ppermute | solution.py:181
  55.9 2.5 %collective-permute-start.3 = (bf16[32,3712]{1,0:T(8,128)(2,1)S(1)}, bf16[32,3712]{1,0:T(8,128)(2,1)S(1)}, u32[]{:S(2)}, u32[]{:S(2)}) collective-permute-start(bf16[32,3712]{1,0:T(8,128)(2,1)S(1)} %collective-permute-done.1.refs_1_), channel_id=1, source_target_pairs={{0,112},{16,0},{32,16},{48,32},{64,48},{80,64},{96,80},{112,96},{1... | collective-permute-start | bytes 712712 | tf_op jit(solution)/shard_map/ppermute | solution.py:181
  58.3 2.2 %collective-permute-start.9 = (bf16[32,3584]{1,0:T(8,128)(2,1)S(1)}, bf16[32,3584]{1,0:T(8,128)(2,1)S(1)}, u32[]{:S(2)}, u32[]{:S(2)}) collective-permute-start(bf16[32,3584]{1,0:T(8,128)(2,1)S(1)} %collective-permute-done.8.refs_11_), channel_id=1, source_target_pairs={{0,112},{16,0},{32,16},{48,32},{64,48},{80,64},{96,80},{112,96},{1... | collective-permute-start | bytes 688136 | tf_op jit(solution)/shard_map/ppermute | solution.py:181
  60.5 4.0 %collective-permute-done.3.refs_3_ = bf16[32,3712]{1,0:T(8,128)(2,1)S(1)} collective-permute-done((bf16[32,3712]{1,0:T(8,128)(2,1)S(1)}, bf16[32,3712]{1,0:T(8,128)(2,1)S(1)}, u32[]{:S(2)}, u32[]{:S(2)}) %collective-permute-start.3) | collective-permute-done | bytes 237600 | tf_op jit(solution)/shard_map/ppermute | solution.py:181
  64.5 2.6 %collective-permute-done.9.refs_13_ = bf16[32,3584]{1,0:T(8,128)(2,1)S(1)} collective-permute-done((bf16[32,3584]{1,0:T(8,128)(2,1)S(1)}, bf16[32,3584]{1,0:T(8,128)(2,1)S(1)}, u32[]{:S(2)}, u32[]{:S(2)}) %collective-permute-start.9) | collective-permute-done | bytes 229408 | tf_op jit(solution)/shard_map/ppermute | solution.py:181
  67.1 6.5 %collective-permute-done.6.refs_6_ = bf16[32,3712]{1,0:T(8,128)(2,1)S(1)} collective-permute-done((bf16[32,3712]{1,0:T(8,128)(2,1)S(1)}, bf16[32,3712]{1,0:T(8,128)(2,1)S(1)}, u32[]{:S(2)}, u32[]{:S(2)}) %collective-permute-start.6) | collective-permute-done | bytes 237600 | tf_op jit(solution)/shard_map/ppermute | solution.py:181
  73.6 3.2 %collective-permute-start.5 = (bf16[32,3712]{1,0:T(8,128)(2,1)S(1)}, bf16[32,3712]{1,0:T(8,128)(2,1)S(1)}, u32[]{:S(2)}, u32[]{:S(2)}) collective-permute-start(bf16[32,3712]{1,0:T(8,128)(2,1)S(1)} %collective-permute-done.3.refs_3_), channel_id=1, source_target_pairs={{0,112},{16,0},{32,16},{48,32},{64,48},{80,64},{96,80},{112,96},{1... | collective-permute-start | bytes 712712 | tf_op jit(solution)/shard_map/ppermute | solution.py:181
  77.2 1.3 collective-permute-done.15.refs_12_
  78.5 3.2 %collective-permute-start.17 = (bf16[32,3584]{1,0:T(8,128)(2,1)S(1)}, bf16[32,3584]{1,0:T(8,128)(2,1)}, u32[]{:S(2)}, u32[]{:S(2)}) collective-permute-start(bf16[32,3584]{1,0:T(8,128)(2,1)S(1)} %collective-permute-done.9.refs_13_), channel_id=1, source_target_pairs={{0,112},{16,0},{32,16},{48,32},{64,48},{80,64},{96,80},{112,96},{1... | collective-permute-start | bytes 688136 | tf_op jit(solution)/shard_map/ppermute | solution.py:181
  81.9 4.2 %shard_map.98 = (bf16[1,7168,256]{2,1,0:T(8,128)(2,1)S(1)}, bf16[1,7168,256]{2,1,0:T(8,128)(2,1)S(1)}, bf16[1,256,7168]{2,1,0:T(8,128)(2,1)S(1)}) custom-call(bf16[1,7168,256]{2,1,0:T(8,128)(2,1)} %collective-permute-done.10.refs_0_, bf16[1,7168,256]{2,1,0:T(8,128)(2,1)} %collective-permute-done.11.refs_1_, bf16[1,256,7168]{2,1,0:T(8,128)(2,1)} %collective-permute-done.12.refs_2_), custom_call_target="tpu_custom_call" | custom-call | flops 5505024 | bytes 22020096 | tf_op jit(solution)/shard_map/pallas_call | solution.py:112
  86.1 1.4 shard_map.97
  87.6 0.7 copy-done.2
  88.2 1.1 fusion.2.refs_4_
  89.4 0.9 copy-done.3
  90.3 1.1 fusion.6.refs_0_
  91.4 1.1 fusion.refs_5_
  92.5 1.1 fusion.4.refs_1_
  93.6 0.9 copy-done
  94.6 2.4 %shard_map.99 = (bf16[128,896]{1,0:T(8,128)(2,1)S(1)}, bf16[128,896]{1,0:T(8,128)(2,1)S(1)}, bf16[128,896]{1,0:T(8,128)(2,1)S(1)}, bf16[128,896]{1,0:T(8,128)(2,...) custom-call(s32[1]{0:T(128)} %bitcast.place, ...), custom_call_target="tpu_custom_call" | custom-call | flops 1879048192 | bytes 7340032 | tf_op jit(solution)/shard_map/pallas_call | solution.py:158
  97.1 3.3 %collective-permute-start.22 = (bf16[64,896]{1,0:T(8,128)(2,1)S(1)}, bf16[64,896]{1,0:T(8,128)(2,1)S(1)}, u32[]{:S(2)}, u32[]{:S(2)}) collective-permute-start(bf16[64,896]{1,0:T(8,128)(2,1)S(1)} %get-tuple-element.45), channel_id=1, source_target_pairs={{0,7},{1,0},{2,1},{3,2},{4,3},{5,4},{6,5},{7,6},{8,15},{9,8},{10,9... | collective-permute-start | bytes 344072 | tf_op jit(solution)/shard_map/ppermute | solution.py:181
  100.6 3.3 %collective-permute-start.30 = (bf16[64,896]{1,0:T(8,128)(2,1)S(1)}, bf16[64,896]{1,0:T(8,128)(2,1)S(1)}, u32[]{:S(2)}, u32[]{:S(2)}) collective-permute-start(bf16[64,896]{1,0:T(8,128)(2,1)S(1)} %get-tuple-element.54), channel_id=1, source_target_pairs={{0,7},{1,0},{2,1},{3,2},{4,3},{5,4},{6,5},{7,6},{8,15},{9,8},{10,9... | collective-permute-start | bytes 344072 | tf_op jit(solution)/shard_map/ppermute | solution.py:181
  104.6 3.5 %collective-permute-start.23 = (bf16[128,896]{1,0:T(8,128)(2,1)S(1)}, bf16[128,896]{1,0:T(8,128)(2,1)S(1)}, u32[]{:S(2)}, u32[]{:S(2)}) collective-permute-start(bf16[128,896]{1,0:T(8,128)(2,1)S(1)} %pad_maximum_fusion.2), channel_id=1, source_target_pairs={{0,7},{1,0},{2,1},{3,2},{4,3},{5,4},{6,5},{7,6},{8,15},{9,8},{10,9... | collective-permute-start | bytes 688136 | tf_op jit(solution)/shard_map/ppermute | solution.py:181
  108.4 3.3 %collective-permute-start.31 = (bf16[128,896]{1,0:T(8,128)(2,1)S(1)}, bf16[128,896]{1,0:T(8,128)(2,1)S(1)}, u32[]{:S(2)}, u32[]{:S(2)}) collective-permute-start(bf16[128,896]{1,0:T(8,128)(2,1)S(1)} %pad_maximum_fusion.4), channel_id=1, source_target_pairs={{0,7},{1,0},{2,1},{3,2},{4,3},{5,4},{6,5},{7,6},{8,15},{9,8},{10,9... | collective-permute-start | bytes 688136 | tf_op jit(solution)/shard_map/ppermute | solution.py:181
  111.7 2.5 %collective-permute-done.19 = bf16[128,896]{1,0:T(8,128)(2,1)S(1)} collective-permute-done((bf16[128,896]{1,0:T(8,128)(2,1)S(1)}, bf16[128,896]{1,0:T(8,128)(2,1)S(1)}, u32[]{:S(2)}, u32[]{:S(2)}) %collective-permute-start.19) | collective-permute-done | bytes 229408 | tf_op jit(solution)/shard_map/ppermute | solution.py:181
  114.5 3.5 %collective-permute-start.24 = (bf16[128,896]{1,0:T(8,128)(2,1)S(1)}, bf16[128,896]{1,0:T(8,128)(2,1)S(1)}, u32[]{:S(2)}, u32[]{:S(2)}) collective-permute-start(bf16[128,896]{1,0:T(8,128)(2,1)S(1)} %add_convert_fusion.7), channel_id=1, source_target_pairs={{0,7},{1,0},{2,1},{3,2},{4,3},{5,4},{6,5},{7,6},{8,15},{9,8},{10,9... | collective-permute-start | bytes 688136 | tf_op jit(solution)/shard_map/ppermute | solution.py:181
  118.0 1.1 collective-permute-done.27
  119.4 3.5 %collective-permute-start.32 = (bf16[128,896]{1,0:T(8,128)(2,1)S(1)}, bf16[128,896]{1,0:T(8,128)(2,1)S(1)}, u32[]{:S(2)}, u32[]{:S(2)}) collective-permute-start(bf16[128,896]{1,0:T(8,128)(2,1)S(1)} %add_convert_fusion.2), channel_id=1, source_target_pairs={{0,7},{1,0},{2,1},{3,2},{4,3},{5,4},{6,5},{7,6},{8,15},{9,8},{10,9... | collective-permute-start | bytes 688136 | tf_op jit(solution)/shard_map/ppermute | solution.py:181
  122.9 1.1 collective-permute-done.20
  124.3 3.5 %collective-permute-start.25 = (bf16[128,896]{1,0:T(8,128)(2,1)S(1)}, bf16[128,896]{1,0:T(8,128)(2,1)S(1)}, u32[]{:S(2)}, u32[]{:S(2)}) collective-permute-start(bf16[128,896]{1,0:T(8,128)(2,1)S(1)} %add_convert_fusion.6), channel_id=1, source_target_pairs={{0,7},{1,0},{2,1},{3,2},{4,3},{5,4},{6,5},{7,6},{8,15},{9,8},{10,9... | collective-permute-start | bytes 688136 | tf_op jit(solution)/shard_map/ppermute | solution.py:181
  128.3 3.3 %collective-permute-start.33 = (bf16[128,896]{1,0:T(8,128)(2,1)S(1)}, bf16[128,896]{1,0:T(8,128)(2,1)S(1)}, u32[]{:S(2)}, u32[]{:S(2)}) collective-permute-start(bf16[128,896]{1,0:T(8,128)(2,1)S(1)} %add_convert_fusion.1), channel_id=1, source_target_pairs={{0,7},{1,0},{2,1},{3,2},{4,3},{5,4},{6,5},{7,6},{8,15},{9,8},{10,9... | collective-permute-start | bytes 688136 | tf_op jit(solution)/shard_map/ppermute | solution.py:181
  131.7 3.7 %collective-permute-done.29 = bf16[128,896]{1,0:T(8,128)(2,1)S(1)} collective-permute-done((bf16[128,896]{1,0:T(8,128)(2,1)S(1)}, bf16[128,896]{1,0:T(8,128)(2,1)S(1)}, u32[]{:S(2)}, u32[]{:S(2)}) %collective-permute-start.29) | collective-permute-done | bytes 229408 | tf_op jit(solution)/shard_map/ppermute | solution.py:181
  135.5 0.8 pad_maximum_fusion
  136.3 7.0 %all-to-all-start = ((bf16[8,32,896]{2,1,0:T(8,128)(2,1)}), bf16[8,32,896]{2,1,0:T(8,128)(2,1)S(1)}, u32[]{:S(2)}, u32[]{:S(2)}) async-start(bf16[8,32,896]{2,1,0:T(8,128)(2,1)} %bitcast.8), calls=%async_computation | async-start | bytes 917504 | tf_op jit(solution)/shard_map/all_to_all | solution.py:237
  143.3 0.5 slice.45
  144.5 10.0 %all-to-all-done = bf16[8,32,896]{2,1,0:T(8,128)(2,1)S(1)} async-done(((bf16[8,32,896]{2,1,0:T(8,128)(2,1)}), bf16[8,32,896]{2,1,0:T(8,128)(2,1)S(1)}, u32[]{:S(2)}, u32[]{:S(2)}) %all-to-all-start) | async-done | bytes 458784 | tf_op jit(solution)/shard_map/all_to_all | solution.py:237
  154.4 0.7 reduce_sum.12
  (68 shorter events, 4.1 us)
Async XLA Ops:
  0.6 76.2 %collective-permute-start.10 = (bf16[1,7168,256]{2,1,0:T(8,128)(2,1)}, bf16[1,7168,256]{2,1,0:T(8,128)(2,1)}, u32[]{:S(2)}, u32[]{:S(2)}) collective-permute-start(bf16[1,7168,256]{2,1,0:T(8,128)(2,1)} %param.9), channel_id=1, source_target_pairs={{0,8},{8,0},{1,9},{9,1},{2,10},{10,2},{3,11},{11,3},{4,12},{12,4},... | collective-permute-start | bytes 11010056 | tf_op jit(solution)/shard_map/ppermute | solution.py:181
  0.8 76.1 %collective-permute-start.11 = (bf16[1,7168,256]{2,1,0:T(8,128)(2,1)}, bf16[1,7168,256]{2,1,0:T(8,128)(2,1)}, u32[]{:S(2)}, u32[]{:S(2)}) collective-permute-start(bf16[1,7168,256]{2,1,0:T(8,128)(2,1)} %param.10), channel_id=1, source_target_pairs={{0,8},{8,0},{1,9},{9,1},{2,10},{10,2},{3,11},{11,3},{4,12},{12,4},... | collective-permute-start | bytes 11010056 | tf_op jit(solution)/shard_map/ppermute | solution.py:181
  1.3 75.6 %collective-permute-start.12 = (bf16[1,256,7168]{2,1,0:T(8,128)(2,1)}, bf16[1,256,7168]{2,1,0:T(8,128)(2,1)}, u32[]{:S(2)}, u32[]{:S(2)}) collective-permute-start(bf16[1,256,7168]{2,1,0:T(8,128)(2,1)} %refs_6_.1), channel_id=1, source_target_pairs={{0,8},{8,0},{1,9},{9,1},{2,10},{10,2},{3,11},{11,3},{4,12},{12,4},... | collective-permute-start | bytes 11010056 | tf_op jit(solution)/shard_map/ppermute | solution.py:181
  2.5 26.5 %collective-permute-start.7 = (bf16[32,3584]{1,0:T(8,128)(2,1)S(1)}, bf16[32,3584]{1,0:T(8,128)(2,1)S(1)}, u32[]{:S(2)}, u32[]{:S(2)}) collective-permute-start(bf16[32,3584]{1,0:T(8,128)(2,1)S(1)} %get-tuple-element.56.refs_8_), channel_id=1, source_target_pairs={{0,112},{16,0},{32,16},{48,32},{64,48},{80,64},{96,80},{112,96},{1... | collective-permute-start | bytes 688136 | tf_op jit(solution)/shard_map/ppermute | solution.py:181
  23.3 1.6 collective-permute-start
  24.8 19.0 %collective-permute-start.14 = (bf16[32,3584]{1,0:T(8,128)(2,1)S(1)}, bf16[32,3584]{1,0:T(8,128)(2,1)S(1)}, u32[]{:S(2)}, u32[]{:S(2)}) collective-permute-start(bf16[32,3584]{1,0:T(8,128)(2,1)S(1)} %get-tuple-element.56.refs_8_), channel_id=1, source_target_pairs={{0,16},{16,32},{32,48},{48,64},{64,80},{80,96},{96,112},{112,0},{1... | collective-permute-start | bytes 688136 | tf_op jit(solution)/shard_map/ppermute | solution.py:181
  27.6 0.7 copy-start.1
  29.0 19.4 %collective-permute-start.2 = (bf16[32,3712]{1,0:T(8,128)(2,1)S(1)}, bf16[32,3712]{1,0:T(8,128)(2,1)S(1)}, u32[]{:S(2)}, u32[]{:S(2)}) collective-permute-start(bf16[32,3712]{1,0:T(8,128)(2,1)S(1)} %shard_map.96.refs_0_), channel_id=1, source_target_pairs={{0,16},{16,32},{32,48},{48,64},{64,80},{80,96},{96,112},{112,0},{1... | collective-permute-start | bytes 712712 | tf_op jit(solution)/shard_map/ppermute | solution.py:181
  43.8 7.5 %collective-permute-start.1 = (bf16[32,3712]{1,0:T(8,128)(2,1)S(1)}, bf16[32,3712]{1,0:T(8,128)(2,1)S(1)}, u32[]{:S(2)}, u32[]{:S(2)}) collective-permute-start(bf16[32,3712]{1,0:T(8,128)(2,1)S(1)} %shard_map.96.refs_0_), channel_id=1, source_target_pairs={{0,112},{16,0},{32,16},{48,32},{64,48},{80,64},{96,80},{112,96},{1... | collective-permute-start | bytes 712712 | tf_op jit(solution)/shard_map/ppermute | solution.py:181
  48.4 7.5 %collective-permute-start.8 = (bf16[32,3584]{1,0:T(8,128)(2,1)S(1)}, bf16[32,3584]{1,0:T(8,128)(2,1)S(1)}, u32[]{:S(2)}, u32[]{:S(2)}) collective-permute-start(bf16[32,3584]{1,0:T(8,128)(2,1)S(1)} %collective-permute-done.7.refs_9_), channel_id=1, source_target_pairs={{0,112},{16,0},{32,16},{48,32},{64,48},{80,64},{96,80},{112,96},{1... | collective-permute-start | bytes 688136 | tf_op jit(solution)/shard_map/ppermute | solution.py:181
  51.3 7.0 %collective-permute-start.4 = (bf16[32,3712]{1,0:T(8,128)(2,1)S(1)}, bf16[32,3712]{1,0:T(8,128)(2,1)S(1)}, u32[]{:S(2)}, u32[]{:S(2)}) collective-permute-start(bf16[32,3712]{1,0:T(8,128)(2,1)S(1)} %collective-permute-done.2.refs_2_), channel_id=1, source_target_pairs={{0,16},{16,32},{32,48},{48,64},{64,80},{80,96},{96,112},{112,0},{1... | collective-permute-start | bytes 712712 | tf_op jit(solution)/shard_map/ppermute | solution.py:181
  55.9 8.7 %collective-permute-start.3 = (bf16[32,3712]{1,0:T(8,128)(2,1)S(1)}, bf16[32,3712]{1,0:T(8,128)(2,1)S(1)}, u32[]{:S(2)}, u32[]{:S(2)}) collective-permute-start(bf16[32,3712]{1,0:T(8,128)(2,1)S(1)} %collective-permute-done.1.refs_1_), channel_id=1, source_target_pairs={{0,112},{16,0},{32,16},{48,32},{64,48},{80,64},{96,80},{112,96},{1... | collective-permute-start | bytes 712712 | tf_op jit(solution)/shard_map/ppermute | solution.py:181
  58.3 8.8 %collective-permute-start.9 = (bf16[32,3584]{1,0:T(8,128)(2,1)S(1)}, bf16[32,3584]{1,0:T(8,128)(2,1)S(1)}, u32[]{:S(2)}, u32[]{:S(2)}) collective-permute-start(bf16[32,3584]{1,0:T(8,128)(2,1)S(1)} %collective-permute-done.8.refs_11_), channel_id=1, source_target_pairs={{0,112},{16,0},{32,16},{48,32},{64,48},{80,64},{96,80},{112,96},{1... | collective-permute-start | bytes 688136 | tf_op jit(solution)/shard_map/ppermute | solution.py:181
  64.5 9.1 %collective-permute-start.6 = (bf16[32,3712]{1,0:T(8,128)(2,1)S(1)}, bf16[32,3712]{1,0:T(8,128)(2,1)S(1)}, u32[]{:S(2)}, u32[]{:S(2)}) collective-permute-start(bf16[32,3712]{1,0:T(8,128)(2,1)S(1)} %collective-permute-done.4.refs_4_), channel_id=1, source_target_pairs={{0,16},{16,32},{32,48},{48,64},{64,80},{80,96},{96,112},{112,0},{1... | collective-permute-start | bytes 712712 | tf_op jit(solution)/shard_map/ppermute | solution.py:181
  67.1 11.4 %collective-permute-start.15 = (bf16[32,3584]{1,0:T(8,128)(2,1)S(1)}, bf16[32,3584]{1,0:T(8,128)(2,1)S(1)}, u32[]{:S(2)}, u32[]{:S(2)}) collective-permute-start(bf16[32,3584]{1,0:T(8,128)(2,1)S(1)} %collective-permute-done.14.refs_10_), channel_id=1, source_target_pairs={{0,16},{16,32},{32,48},{48,64},{64,80},{80,96},{96,112},{112,0},{1... | collective-permute-start | bytes 688136 | tf_op jit(solution)/shard_map/ppermute | solution.py:181
  73.6 12.5 %collective-permute-start.5 = (bf16[32,3712]{1,0:T(8,128)(2,1)S(1)}, bf16[32,3712]{1,0:T(8,128)(2,1)S(1)}, u32[]{:S(2)}, u32[]{:S(2)}) collective-permute-start(bf16[32,3712]{1,0:T(8,128)(2,1)S(1)} %collective-permute-done.3.refs_3_), channel_id=1, source_target_pairs={{0,112},{16,0},{32,16},{48,32},{64,48},{80,64},{96,80},{112,96},{1... | collective-permute-start | bytes 712712 | tf_op jit(solution)/shard_map/ppermute | solution.py:181
  76.9 9.3 %collective-permute-start.13 = (bf16[32,3712]{1,0:T(8,128)(2,1)S(1)}, bf16[32,3712]{1,0:T(8,128)(2,1)S(1)}, u32[]{:S(2)}, u32[]{:S(2)}) collective-permute-start(bf16[32,3712]{1,0:T(8,128)(2,1)S(1)} %collective-permute-done.6.refs_6_), channel_id=1, source_target_pairs={{0,16},{16,32},{32,48},{48,64},{64,80},{80,96},{96,112},{112,0},{1... | collective-permute-start | bytes 712712 | tf_op jit(solution)/shard_map/ppermute | solution.py:181
  78.5 7.6 %collective-permute-start.16 = (bf16[32,3584]{1,0:T(8,128)(2,1)S(1)}, bf16[32,3584]{1,0:T(8,128)(2,1)S(1)}, u32[]{:S(2)}, u32[]{:S(2)}) collective-permute-start(bf16[32,3584]{1,0:T(8,128)(2,1)S(1)} %collective-permute-done.15.refs_12_), channel_id=1, source_target_pairs={{0,16},{16,32},{32,48},{48,64},{64,80},{80,96},{96,112},{112,0},{1... | collective-permute-start | bytes 688136 | tf_op jit(solution)/shard_map/ppermute | solution.py:181
  78.5 7.6 %collective-permute-start.17 = (bf16[32,3584]{1,0:T(8,128)(2,1)S(1)}, bf16[32,3584]{1,0:T(8,128)(2,1)}, u32[]{:S(2)}, u32[]{:S(2)}) collective-permute-start(bf16[32,3584]{1,0:T(8,128)(2,1)S(1)} %collective-permute-done.9.refs_13_), channel_id=1, source_target_pairs={{0,112},{16,0},{32,16},{48,32},{64,48},{80,64},{96,80},{112,96},{1... | collective-permute-start | bytes 688136 | tf_op jit(solution)/shard_map/ppermute | solution.py:181
  86.1 2.2 %copy-start.2 = (bf16[1,7168,256]{2,1,0:T(8,128)(2,1)S(1)}, bf16[1,7168,256]{2,1,0:T(8,128)(2,1)}, u32[]{:S(2)}) copy-start(bf16[1,7168,256]{2,1,0:T(8,128)(2,1)} %param.10) | copy-start | bytes 11010052
  88.2 2.0 %copy-start.3 = (bf16[1,7168,256]{2,1,0:T(8,128)(2,1)S(1)}, bf16[1,7168,256]{2,1,0:T(8,128)(2,1)}, u32[]{:S(2)}) copy-start(bf16[1,7168,256]{2,1,0:T(8,128)(2,1)} %param.9) | copy-start | bytes 11010052
  92.5 2.0 %copy-start = (bf16[1,256,7168]{2,1,0:T(8,128)(2,1)S(1)}, bf16[1,256,7168]{2,1,0:T(8,128)(2,1)}, u32[]{:S(2)}) copy-start(bf16[1,256,7168]{2,1,0:T(8,128)(2,1)} %refs_6_.1) | copy-start | bytes 11010052
  97.0 7.3 %collective-permute-start.18 = (bf16[64,896]{1,0:T(8,128)(2,1)S(1)}, bf16[64,896]{1,0:T(8,128)(2,1)S(1)}, u32[]{:S(2)}, u32[]{:S(2)}) collective-permute-start(bf16[64,896]{1,0:T(8,128)(2,1)S(1)} %get-tuple-element.41), channel_id=1, source_target_pairs={{0,1},{1,2},{2,3},{3,4},{4,5},{5,6},{6,7},{7,0},{8,9},{9,10},{10,1... | collective-permute-start | bytes 344072 | tf_op jit(solution)/shard_map/ppermute | solution.py:181
  97.1 7.4 %collective-permute-start.22 = (bf16[64,896]{1,0:T(8,128)(2,1)S(1)}, bf16[64,896]{1,0:T(8,128)(2,1)S(1)}, u32[]{:S(2)}, u32[]{:S(2)}) collective-permute-start(bf16[64,896]{1,0:T(8,128)(2,1)S(1)} %get-tuple-element.45), channel_id=1, source_target_pairs={{0,7},{1,0},{2,1},{3,2},{4,3},{5,4},{6,5},{7,6},{8,15},{9,8},{10,9... | collective-permute-start | bytes 344072 | tf_op jit(solution)/shard_map/ppermute | solution.py:181
  100.5 7.7 %collective-permute-start.26 = (bf16[64,896]{1,0:T(8,128)(2,1)S(1)}, bf16[64,896]{1,0:T(8,128)(2,1)S(1)}, u32[]{:S(2)}, u32[]{:S(2)}) collective-permute-start(bf16[64,896]{1,0:T(8,128)(2,1)S(1)} %get-tuple-element.50), channel_id=1, source_target_pairs={{0,1},{1,2},{2,3},{3,4},{4,5},{5,6},{6,7},{7,0},{8,9},{9,10},{10,1... | collective-permute-start | bytes 344072 | tf_op jit(solution)/shard_map/ppermute | solution.py:181
  100.6 7.7 %collective-permute-start.30 = (bf16[64,896]{1,0:T(8,128)(2,1)S(1)}, bf16[64,896]{1,0:T(8,128)(2,1)S(1)}, u32[]{:S(2)}, u32[]{:S(2)}) collective-permute-start(bf16[64,896]{1,0:T(8,128)(2,1)S(1)} %get-tuple-element.54), channel_id=1, source_target_pairs={{0,7},{1,0},{2,1},{3,2},{4,3},{5,4},{6,5},{7,6},{8,15},{9,8},{10,9... | collective-permute-start | bytes 344072 | tf_op jit(solution)/shard_map/ppermute | solution.py:181
  104.4 9.8 %collective-permute-start.19 = (bf16[128,896]{1,0:T(8,128)(2,1)S(1)}, bf16[128,896]{1,0:T(8,128)(2,1)S(1)}, u32[]{:S(2)}, u32[]{:S(2)}) collective-permute-start(bf16[128,896]{1,0:T(8,128)(2,1)S(1)} %pad_maximum_fusion.1), channel_id=1, source_target_pairs={{0,1},{1,2},{2,3},{3,4},{4,5},{5,6},{6,7},{7,0},{8,9},{9,10},{10,1... | collective-permute-start | bytes 688136 | tf_op jit(solution)/shard_map/ppermute | solution.py:181
  104.6 9.8 %collective-permute-start.23 = (bf16[128,896]{1,0:T(8,128)(2,1)S(1)}, bf16[128,896]{1,0:T(8,128)(2,1)S(1)}, u32[]{:S(2)}, u32[]{:S(2)}) collective-permute-start(bf16[128,896]{1,0:T(8,128)(2,1)S(1)} %pad_maximum_fusion.2), channel_id=1, source_target_pairs={{0,7},{1,0},{2,1},{3,2},{4,3},{5,4},{6,5},{7,6},{8,15},{9,8},{10,9... | collective-permute-start | bytes 688136 | tf_op jit(solution)/shard_map/ppermute | solution.py:181
  108.2 10.9 %collective-permute-start.27 = (bf16[128,896]{1,0:T(8,128)(2,1)S(1)}, bf16[128,896]{1,0:T(8,128)(2,1)S(1)}, u32[]{:S(2)}, u32[]{:S(2)}) collective-permute-start(bf16[128,896]{1,0:T(8,128)(2,1)S(1)} %pad_maximum_fusion.3), channel_id=1, source_target_pairs={{0,1},{1,2},{2,3},{3,4},{4,5},{5,6},{6,7},{7,0},{8,9},{9,10},{10,1... | collective-permute-start | bytes 688136 | tf_op jit(solution)/shard_map/ppermute | solution.py:181
  108.4 10.9 %collective-permute-start.31 = (bf16[128,896]{1,0:T(8,128)(2,1)S(1)}, bf16[128,896]{1,0:T(8,128)(2,1)S(1)}, u32[]{:S(2)}, u32[]{:S(2)}) collective-permute-start(bf16[128,896]{1,0:T(8,128)(2,1)S(1)} %pad_maximum_fusion.4), channel_id=1, source_target_pairs={{0,7},{1,0},{2,1},{3,2},{4,3},{5,4},{6,5},{7,6},{8,15},{9,8},{10,9... | collective-permute-start | bytes 688136 | tf_op jit(solution)/shard_map/ppermute | solution.py:181
  114.2 9.8 %collective-permute-start.20 = (bf16[128,896]{1,0:T(8,128)(2,1)S(1)}, bf16[128,896]{1,0:T(8,128)(2,1)S(1)}, u32[]{:S(2)}, u32[]{:S(2)}) collective-permute-start(bf16[128,896]{1,0:T(8,128)(2,1)S(1)} %add_convert_fusion.9), channel_id=1, source_target_pairs={{0,1},{1,2},{2,3},{3,4},{4,5},{5,6},{6,7},{7,0},{8,9},{9,10},{10,1... | collective-permute-start | bytes 688136 | tf_op jit(solution)/shard_map/ppermute | solution.py:181
  114.5 9.8 %collective-permute-start.24 = (bf16[128,896]{1,0:T(8,128)(2,1)S(1)}, bf16[128,896]{1,0:T(8,128)(2,1)S(1)}, u32[]{:S(2)}, u32[]{:S(2)}) collective-permute-start(bf16[128,896]{1,0:T(8,128)(2,1)S(1)} %add_convert_fusion.7), channel_id=1, source_target_pairs={{0,7},{1,0},{2,1},{3,2},{4,3},{5,4},{6,5},{7,6},{8,15},{9,8},{10,9... | collective-permute-start | bytes 688136 | tf_op jit(solution)/shard_map/ppermute | solution.py:181
  119.2 8.9 %collective-permute-start.28 = (bf16[128,896]{1,0:T(8,128)(2,1)S(1)}, bf16[128,896]{1,0:T(8,128)(2,1)S(1)}, u32[]{:S(2)}, u32[]{:S(2)}) collective-permute-start(bf16[128,896]{1,0:T(8,128)(2,1)S(1)} %add_convert_fusion.4), channel_id=1, source_target_pairs={{0,1},{1,2},{2,3},{3,4},{4,5},{5,6},{6,7},{7,0},{8,9},{9,10},{10,1... | collective-permute-start | bytes 688136 | tf_op jit(solution)/shard_map/ppermute | solution.py:181
  119.4 8.9 %collective-permute-start.32 = (bf16[128,896]{1,0:T(8,128)(2,1)S(1)}, bf16[128,896]{1,0:T(8,128)(2,1)S(1)}, u32[]{:S(2)}, u32[]{:S(2)}) collective-permute-start(bf16[128,896]{1,0:T(8,128)(2,1)S(1)} %add_convert_fusion.2), channel_id=1, source_target_pairs={{0,7},{1,0},{2,1},{3,2},{4,3},{5,4},{6,5},{7,6},{8,15},{9,8},{10,9... | collective-permute-start | bytes 688136 | tf_op jit(solution)/shard_map/ppermute | solution.py:181
  124.1 7.5 %collective-permute-start.21 = (bf16[128,896]{1,0:T(8,128)(2,1)S(1)}, bf16[128,896]{1,0:T(8,128)(2,1)S(1)}, u32[]{:S(2)}, u32[]{:S(2)}) collective-permute-start(bf16[128,896]{1,0:T(8,128)(2,1)S(1)} %add_convert_fusion.8), channel_id=1, source_target_pairs={{0,1},{1,2},{2,3},{3,4},{4,5},{5,6},{6,7},{7,0},{8,9},{9,10},{10,1... | collective-permute-start | bytes 688136 | tf_op jit(solution)/shard_map/ppermute | solution.py:181
  124.3 7.3 %collective-permute-start.25 = (bf16[128,896]{1,0:T(8,128)(2,1)S(1)}, bf16[128,896]{1,0:T(8,128)(2,1)S(1)}, u32[]{:S(2)}, u32[]{:S(2)}) collective-permute-start(bf16[128,896]{1,0:T(8,128)(2,1)S(1)} %add_convert_fusion.6), channel_id=1, source_target_pairs={{0,7},{1,0},{2,1},{3,2},{4,3},{5,4},{6,5},{7,6},{8,15},{9,8},{10,9... | collective-permute-start | bytes 688136 | tf_op jit(solution)/shard_map/ppermute | solution.py:181
  128.1 7.3 %collective-permute-start.29 = (bf16[128,896]{1,0:T(8,128)(2,1)S(1)}, bf16[128,896]{1,0:T(8,128)(2,1)S(1)}, u32[]{:S(2)}, u32[]{:S(2)}) collective-permute-start(bf16[128,896]{1,0:T(8,128)(2,1)S(1)} %add_convert_fusion.3), channel_id=1, source_target_pairs={{0,1},{1,2},{2,3},{3,4},{4,5},{5,6},{6,7},{7,0},{8,9},{9,10},{10,1... | collective-permute-start | bytes 688136 | tf_op jit(solution)/shard_map/ppermute | solution.py:181
  128.3 7.1 %collective-permute-start.33 = (bf16[128,896]{1,0:T(8,128)(2,1)S(1)}, bf16[128,896]{1,0:T(8,128)(2,1)S(1)}, u32[]{:S(2)}, u32[]{:S(2)}) collective-permute-start(bf16[128,896]{1,0:T(8,128)(2,1)S(1)} %add_convert_fusion.1), channel_id=1, source_target_pairs={{0,7},{1,0},{2,1},{3,2},{4,3},{5,4},{6,5},{7,6},{8,15},{9,8},{10,9... | collective-permute-start | bytes 688136 | tf_op jit(solution)/shard_map/ppermute | solution.py:181
  136.3 18.1 %all-to-all-start = ((bf16[8,32,896]{2,1,0:T(8,128)(2,1)}), bf16[8,32,896]{2,1,0:T(8,128)(2,1)S(1)}, u32[]{:S(2)}, u32[]{:S(2)}) async-start(bf16[8,32,896]{2,1,0:T(8,128)(2,1)} %bitcast.8), calls=%async_computation | async-start | bytes 917504 | tf_op jit(solution)/shard_map/all_to_all | solution.py:237
